TPU v7x, 256 devices: a whole 4x4x8 slice. The times are simulated.
256 devices in a mesh: dp: 256 (over z, y, x, core).
Axes of the slice: x: 4, y: 4, z: 8, core: 2. Of those that a mesh axis runs over, the one named last changes fastest.
Arguments:
- tokens: bfloat16 [262144, 1024], P('dp'), may hold values from -80 to 80
- seg_ids: int32 [256, 1024], P('dp'), may hold values from 0 to 3, as said below
- counts: int32 [256], replicated, may hold values from 1 to 4, as said below
- positives: int32 [1024], P('dp'), may hold values from 0 to 1023, as said below
- w_qkv: bfloat16 [1024, 1536], replicated, may hold values from -0.1875 to 0.1875
- w_out: bfloat16 [512, 1024], replicated, may hold values from -0.25 to 0.25
- ln_gain: float32 [1024], replicated, may hold values from 0.1 to 1.9
- w_proj: bfloat16 [1024, 2048], replicated, may hold values from -0.1875 to 0.1875
Outputs:
- loss: float32 [1024], P('dp')
- grad_pooled: float32 [1024, 1024], P('dp')
Inputs may be any that keep to these rules, and one draw needn't show every extreme that they name: `seg_ids`: within a rank, the ids never fall and every id from 0 to 3 occurs. Rank r's live segments are its slots 0 to counts[r] - 1; the other slots hold padding; some rank has all 4 live. `positives`: a live slot of another rank, as rank times 4 plus slot.
All inputs are finite; a program needn't handle non-finite values.
Results may differ from a plain program's by a relative error of at most 0.008.
Values may be sent and summed in bfloat16 or wider, within the bound.
A program may use at most 192 MiB of HBM per device.

v0:
```python
import jax
import jax.numpy as jnp
from jax import lax
from jax.sharding import Mesh
from jax.sharding import PartitionSpec as P

HEADS = 8
DP = ("dp_0", "dp_1", "dp_2", "dp_3")


logit_scale = 20.0


def from_everyone(shard, axis):
    copies = jnp.broadcast_to(shard, (lax.axis_size(axis), *shard.shape))
    return lax.all_to_all(copies, axis, split_axis=0, concat_axis=0, tiled=True)


def joined_along(pieces, dim):
    lengths = list(pieces.shape[1:])
    lengths[dim] *= pieces.shape[0]
    return jnp.moveaxis(pieces, 0, dim).reshape(lengths)


def gathered_by_axis(shard, axes, dim):
    far, near = axes
    leading = from_everyone(shard, far)
    pieces = jnp.swapaxes(from_everyone(leading, near), 0, 1)
    return joined_along(pieces.reshape(-1, *shard.shape), dim)


def attend(tok_rows, segment, w_qkv, w_out, ln_gain):
    rows = tok_rows.shape[0]
    width = w_out.shape[0]
    head_dim = width // HEADS
    qkv = jnp.dot(tok_rows, w_qkv, preferred_element_type=jnp.float32).astype(jnp.bfloat16)
    qkv = qkv.reshape(rows, 3, HEADS, head_dim)
    queries_all = qkv[:, 0]
    keys_all = qkv[:, 1]
    values_all = qkv[:, 2]
    block_rows = min(512, rows)
    pieces = []
    for row_begin in range(0, rows, block_rows):
        query_block = queries_all[row_begin : row_begin + block_rows]
        scores = jnp.einsum(
            "qhd,khd->hqk", query_block, keys_all, preferred_element_type=jnp.float32
        )
        scores = scores * head_dim ** (-0.5)
        same = segment[row_begin : row_begin + block_rows, None] == segment[None, :]
        scores = jnp.where(same[None], scores, -1e30)
        row_max = jnp.max(scores, axis=-1, keepdims=True)
        exp_scores = jnp.exp(scores - row_max)
        probs = (exp_scores / jnp.sum(exp_scores, axis=-1, keepdims=True)).astype(jnp.bfloat16)
        context = jnp.einsum("hqk,khd->qhd", probs, values_all, preferred_element_type=jnp.float32)
        pieces.append(context.astype(jnp.bfloat16).reshape(block_rows, width))
    context = jnp.concatenate(pieces, axis=0)
    resid = tok_rows.astype(jnp.float32) + jnp.dot(
        context, w_out, preferred_element_type=jnp.float32
    )
    centre = resid - jnp.mean(resid, axis=-1, keepdims=True)
    variance = jnp.mean(centre * centre, axis=-1, keepdims=True)
    return (centre * lax.rsqrt(variance + 1e-05) * ln_gain).astype(jnp.bfloat16)


def pool_rows(hidden, segment, slots):
    member = jnp.arange(slots, dtype=jnp.int32)[:, None] == segment[None, :]
    sums = jnp.dot(member.astype(jnp.bfloat16), hidden, preferred_element_type=jnp.float32)
    sizes = jnp.sum(member.astype(jnp.float32), axis=1, keepdims=True)
    return (sums / sizes).astype(jnp.bfloat16)


def embed_rows(pooled, w_proj):
    proj = jnp.dot(pooled, w_proj, preferred_element_type=jnp.float32)
    rnorm = lax.rsqrt(jnp.sum(proj * proj, axis=-1, keepdims=True) + 1e-06)
    return (proj * rnorm, rnorm)


def body(tokens, seg_ids, counts, positives, w_qkv, w_out, ln_gain, w_proj):
    my_rank = lax.axis_index(DP)
    devices = lax.axis_size(DP)
    segment = seg_ids[0]
    slots = positives.shape[0]
    all_slots = slots * devices
    hidden = attend(tokens, segment, w_qkv, w_out, ln_gain)
    pooled = pool_rows(hidden, segment, slots)
    unit, rnorm = embed_rows(pooled, w_proj)
    emb = unit.astype(jnp.bfloat16)
    all_pooled = gathered_by_axis(pooled, (("dp_0", "dp_1"), ("dp_2", "dp_3")), 0)
    all_unit, all_rnorm = embed_rows(all_pooled, w_proj)
    all_emb = all_unit.astype(jnp.bfloat16)
    slot_ids = jnp.arange(all_slots, dtype=jnp.int32)
    own_ids = my_rank * slots + jnp.arange(slots, dtype=jnp.int32)
    live_counts = jnp.broadcast_to(counts[:, None], (devices, slots)).reshape(all_slots)
    live = slot_ids % slots < live_counts
    my_count = lax.dynamic_index_in_dim(counts, my_rank, 0, keepdims=False)
    live_query = jnp.arange(slots, dtype=jnp.int32) < my_count
    logits = logit_scale * lax.dot_general(
        emb, all_emb, (((1,), (1,)), ((), ())), preferred_element_type=jnp.float32
    )
    allowed = live[None, :] & (slot_ids[None, :] != own_ids[:, None])
    exp_logits = jnp.where(allowed, jnp.exp(logits), 0.0)
    denominator = jnp.sum(exp_logits, axis=-1)
    target = slot_ids[None, :] == positives[:, None]
    picked = jnp.sum(jnp.where(target, logits, 0.0), axis=-1)
    loss = jnp.where(live_query, jnp.log(denominator) - picked, 0.0)
    weights = jnp.where(
        live_query[:, None], exp_logits / denominator[:, None] - target.astype(jnp.float32), 0.0
    )
    weights = weights.astype(jnp.bfloat16)
    d_query = logit_scale * jnp.dot(weights, all_emb, preferred_element_type=jnp.float32)
    all_denominator, all_targets = (
        gathered_by_axis(denominator, (("dp_0", "dp_1"), ("dp_2", "dp_3")), 0),
        gathered_by_axis(positives.astype(jnp.float32), (("dp_0", "dp_1"), ("dp_2", "dp_3")), 0),
    )
    all_positives = all_targets.astype(jnp.int32)
    column_logits = logit_scale * lax.dot_general(
        all_emb, emb, (((1,), (1,)), ((), ())), preferred_element_type=jnp.float32
    )
    column_allowed = live_query[None, :] & (slot_ids[:, None] != own_ids[None, :])
    column_exp = jnp.where(column_allowed, jnp.exp(column_logits), 0.0)
    column_hits = (all_positives[:, None] == own_ids[None, :]).astype(jnp.float32)
    column_weights = jnp.where(
        live[:, None], column_exp / all_denominator[:, None] - column_hits, 0.0
    )
    column_weights = column_weights.astype(jnp.bfloat16)
    d_key = logit_scale * lax.dot_general(
        column_weights, all_emb, (((0,), (0,)), ((), ())), preferred_element_type=jnp.float32
    )
    d_emb = d_query + d_key
    radial = jnp.sum(d_emb * unit, axis=-1, keepdims=True)
    d_proj = ((d_emb - radial * unit) * rnorm).astype(jnp.bfloat16)
    grad_pooled = lax.dot_general(
        d_proj, w_proj, (((1,), (1,)), ((), ())), preferred_element_type=jnp.float32
    )
    return (loss, grad_pooled)


def solution(mesh):
    finer = Mesh(mesh.devices.reshape(8, 4, 4, 2), ("dp_0", "dp_1", "dp_2", "dp_3"))
    return jax.shard_map(
        body,
        mesh=finer,
        in_specs=(P(DP, None), P(DP, None), P(), P(DP), P(), P(), P(), P()),
        out_specs=(P(DP), P(DP, None)),
        check_vma=False,
    )
```

profile of v0, /device:TPU:1, one launch (start us, length us, event | category | flops | bytes accessed | tf_op | source)
XLA Modules:
  0.0 223.1 jit_solution(16379266633564425066)
XLA Ops:
  2.1 12.0 %all-to-all-start.4 = ((f32[32,1,4]{2,1,0:T(1,128)}), f32[32,1,4]{2,1,0:T(1,128)S(1)}, u32[]{:S(2)}, u32[]{:S(2)}) async-start(f32[32,1,4]{2,1,0:T(1,128)} %broadcast_in_dim.117), calls=%async_computation.4 | async-start | bytes 32768 | tf_op jit(solution)/shard_map/all_to_all | solution.py:16
  14.1 6.4 %convolution_convert_fusion = bf16[1024,1536]{1,0:T(8,128)(2,1)} fusion(bf16[1024,1024]{1,0:T(8,128)(2,1)} %param.8, bf16[1024,1536]{1,0:T(8,128)(2,1)S(1)} %copy-done), kind=kOutput, calls=%fused_computation.23 | convolution fusion | flops 3222798336 | bytes 8388608 | tf_op jit(solution)/shard_map/dot_general | solution.py:36
  20.5 3.2 %copy.29 = bf16[1024,1536]{0,1:T(8,128)(2,1)S(1)} copy(bf16[1024,1536]{1,0:T(8,128)(2,1)} %convolution_convert_fusion) | data formatting | bytes 6291456 | tf_op jit(solution)/shard_map/convert_element_type | solution.py:36
  23.7 8.1 %fusion.28 = f32[8,512,1024]{2,1,0:T(8,128)} fusion(bf16[1024,3,8,64]{0,3,2,1:T(8,128)(2,1)S(1)} %bitcast.52), kind=kOutput, calls=%fused_computation.47 | convolution fusion | flops 536870912 | bytes 18350080 | tf_op jit(solution)/shard_map/qhd,khd->hqk/dot_general | solution.py:45
  31.8 8.1 %fusion.27 = f32[8,512,1024]{2,1,0:T(8,128)} fusion(bf16[1024,3,8,64]{0,3,2,1:T(8,128)(2,1)S(1)} %bitcast.53), kind=kOutput, calls=%fused_computation.46 | convolution fusion | flops 536870912 | bytes 18350080 | tf_op jit(solution)/shard_map/qhd,khd->hqk/dot_general | solution.py:45
  39.9 3.9 %copy.28 = bf16[1024,1024]{0,1:T(8,128)(2,1)} copy(bf16[1024,1024]{1,0:T(8,128)(2,1)} %param.8) | data formatting | bytes 4194304 | tf_op args[0]
  45.5 21.6 %fusion.67 = (f32[8,512]{1,0:T(8,128)S(1)}, f32[8,512,1024]{2,1,0:T(8,128)}) fusion(f32[8,512,1024]{2,1,0:T(8,128)} %fusion.28, pred[512,1024]{1,0:T(8,128)(4,1)} %get-tuple-element.4), kind=kOutput, calls=%fused_computation.110 | output fusion | flops 25166848 | bytes 34095104 | tf_op jit(solution)/shard_map/sub | solution.py:52
  67.0 7.9 %fusion.15 = bf16[8,64,512]{2,1,0:T(8,128)(2,1)} fusion(f32[8,512,1024]{2,1,0:T(8,128)} %get-tuple-element.11, f32[8,512]{1,0:T(8,128)S(1)} %get-tuple-element.10, bf16[1024,3,8,64]{0,3,2,1:T(8,128)(2,1)S(1)} %bitcast.54), kind=kOutput, calls=%fused_computation.28 | convolution fusion | flops 545521664 | bytes 18366464 | tf_op jit(solution)/shard_map/hqk,khd->qhd/dot_general | solution.py:54
  75.0 21.7 %fusion.66 = (f32[8,512]{1,0:T(8,128)S(1)}, f32[8,512,1024]{2,1,0:T(8,128)}) fusion(f32[8,512,1024]{2,1,0:T(8,128)} %fusion.27, pred[512,1024]{1,0:T(8,128)(4,1)} %get-tuple-element.5), kind=kOutput, calls=%fused_computation.109 | output fusion | flops 25166848 | bytes 34095104 | tf_op jit(solution)/shard_map/sub | solution.py:52
  96.6 7.4 %fusion.14 = bf16[8,64,512]{2,1,0:T(8,128)(2,1)S(1)} fusion(f32[8,512,1024]{2,1,0:T(8,128)} %get-tuple-element.9, f32[8,512]{1,0:T(8,128)S(1)} %get-tuple-element.8, bf16[1024,3,8,64]{0,3,2,1:T(8,128)(2,1)S(1)} %bitcast.55), kind=kOutput, calls=%fused_computation.27 | convolution fusion | flops 545521664 | bytes 18366464 | tf_op jit(solution)/shard_map/hqk,khd->qhd/dot_general | solution.py:54
  108.8 5.3 %all-to-all-start.5 = ((f32[8,1,128]{2,1,0:T(1,128)}), f32[8,1,128]{2,1,0:T(1,128)S(1)}, u32[]{:S(2)}, u32[]{:S(2)}) async-start(f32[8,1,128]{2,1,0:T(1,128)} %reshape.179), calls=%async_computation.5 | async-start | bytes 8192 | tf_op jit(solution)/shard_map/all_to_all | solution.py:16
  114.1 2.9 %fusion.23 = bf16[4,1024]{1,0:T(4,128)(2,1)S(1)} fusion(f32[1024,1024]{0,1:T(8,128)} %copy-done.3, f32[1024]{0:T(1024)S(1)} %copy-done.6, f32[1024]{0:T(1024)S(1)} %add_rsqrt_fusion.1, f32[1024]{0:T(1024)S(1)} %broadcast_multiply_fusion, f32[4]{0:T(128)S(1)} %convert_reduce_fusion, s32[1024]{0:T(1024)S(1)} %bitcast.59), kind=kOutput, calls=%fused_computation.38 | convolution fusion | flops 12595200 | bytes 4218896 | tf_op jit(solution)/shard_map/dot_general | solution.py:67
  118.7 20.6 %all_to_all.38 = bf16[32,4,1024]{2,1,0:T(4,128)(2,1)S(1)} all-to-all(bf16[32,4,1024]{2,1,0:T(4,128)(2,1)S(1)} %broadcast_in_dim.108), channel_id=1, replica_groups=mesh['dp_0'=8,'dp_1'=4,'dp_2'=4,'dp_3'=2] {'dp_0','dp_1'}, dimensions={0} | all-to-all | bytes 524288 | tf_op jit(solution)/shard_map/all_to_all | solution.py:16
  141.3 6.0 %all-to-all-start.1 = ((bf16[8,32,4,1024]{3,2,1,0:T(4,128)(2,1)}), bf16[8,32,4,1024]{3,2,1,0:T(4,128)(2,1)S(1)}, u32[]{:S(2)}, u32[]{:S(2)}) async-start(bf16[8,32,4,1024]{3,2,1,0:T(4,128)(2,1)} %broadcast_in_dim.109), calls=%async_computation.1 | async-start | bytes 4194304 | tf_op jit(solution)/shard_map/all_to_all | solution.py:16
  148.8 3.0 %multiply_reduce_fusion.3 = (f32[4]{0:T(128)S(1)}, f32[4,2048]{1,0:T(4,128)S(1)}) fusion(bf16[4,1024]{1,0:T(4,128)(2,1)S(1)} %fusion.23, bf16[1024,2048]{1,0:T(8,128)(2,1)} %param.15), kind=kOutput, calls=%fused_computation.52 | convolution fusion | flops 16793596 | bytes 4235280 | tf_op jit(solution)/shard_map/dot_general | solution.py:73
  153.3 20.3 %all-to-all-done.1 = bf16[8,32,4,1024]{3,2,1,0:T(4,128)(2,1)S(1)} async-done(((bf16[8,32,4,1024]{3,2,1,0:T(4,128)(2,1)}), bf16[8,32,4,1024]{3,2,1,0:T(4,128)(2,1)S(1)}, u32[]{:S(2)}, u32[]{:S(2)}) %all-to-all-start.1) | async-done | bytes 2097184 | tf_op jit(solution)/shard_map/all_to_all | solution.py:16
  178.6 6.4 %multiply_reduce_fusion = (f32[1024]{0:T(1024)S(1)}, f32[1024,2048]{1,0:T(8,128)S(1)}) fusion(bf16[1024,1024]{1,0:T(8,128)(2,1)S(1)} %reshape_reshape.4, bf16[1024,2048]{1,0:T(8,128)(2,1)} %param.15), kind=kOutput, calls=%fused_computation.11 | convolution fusion | flops 4299160576 | bytes 14684160 | tf_op jit(solution)/shard_map/dot_general | solution.py:73
  189.4 3.8 %all-to-all-start.2 = ((f32[32,1,4]{2,1,0:T(1,128)}), f32[32,1,4]{2,1,0:T(1,128)S(1)}, u32[]{:S(2)}, u32[]{:S(2)}) async-start(f32[32,1,4]{2,1,0:T(1,128)} %broadcast_in_dim.115), calls=%async_computation.2 | async-start | bytes 32768 | tf_op jit(solution)/shard_map/all_to_all | solution.py:16
  193.3 2.9 %fusion.38 = f32[4,2048]{1,0:T(4,128)S(1)} fusion(bf16[1024,2048]{1,0:T(8,128)(2,1)} %copy-done.2, f32[4,1024]{1,0:T(4,128)S(1)} %get-tuple-element.18, f32[4]{0:T(128)S(1)} %get-tuple-element.2, s32[4]{0:T(128)S(1)} %copy-done.7, s32[4]{0:T(128)S(1)} %iota_add_fusion, pred[4]{0:T(512)(128)(4,1)S(1)} %iota_compare_fusion.5, pred[1024]{0:T(1024)(128)(4,1)S(1)} %fusion.53), kind=kOutput, calls=%fused_computation.72 | convolution fusion | flops 16814080 | bytes 4244532 | tf_op jit(solution)/shard_map/dot_general | solution.py:110
  196.2 5.7 %all-to-all-done.2 = f32[32,1,4]{2,1,0:T(1,128)S(1)} async-done(((f32[32,1,4]{2,1,0:T(1,128)}), f32[32,1,4]{2,1,0:T(1,128)S(1)}, u32[]{:S(2)}, u32[]{:S(2)}) %all-to-all-start.2) | async-done | bytes 544 | tf_op jit(solution)/shard_map/all_to_all | solution.py:16
  202.6 5.5 %all-to-all-start.3 = ((f32[8,1,128]{2,1,0:T(1,128)}), f32[8,1,128]{2,1,0:T(1,128)S(1)}, u32[]{:S(2)}, u32[]{:S(2)}) async-start(f32[8,1,128]{2,1,0:T(1,128)} %reshape.181), calls=%async_computation.3 | async-start | bytes 8192 | tf_op jit(solution)/shard_map/all_to_all | solution.py:16
  209.2 3.4 %all-to-all-done.3 = f32[8,1,128]{2,1,0:T(1,128)S(1)} async-done(((f32[8,1,128]{2,1,0:T(1,128)}), f32[8,1,128]{2,1,0:T(1,128)S(1)}, u32[]{:S(2)}, u32[]{:S(2)}) %all-to-all-start.3) | async-done | bytes 4128 | tf_op jit(solution)/shard_map/all_to_all | solution.py:16
  213.6 5.5 %multiply_reduce_fusion.2 = (f32[4]{0:T(128)S(1)}, f32[4,2048]{1,0:T(4,128)S(1)}) fusion(f32[4,2048]{1,0:T(4,128)S(1)} %get-tuple-element.17, f32[4]{0:T(128)S(1)} %add_rsqrt_fusion.2, f32[4,2048]{1,0:T(4,128)S(1)} %fusion.38, bf16[1024,2048]{1,0:T(8,128)(2,1)} %copy-done.2, s32[1024]{0:T(1024)S(1)} %convert_element_type.89, f32[1024]{0:T(1024)S(1)} %div.58, ...), kind=kOutput, calls=%fused_computation.51 | convolution fusion | flops 33652732 | bytes 4301876 | tf_op jit(solution)/shard_map/dot_general | solution.py:126
  219.1 4.0 %fusion.29 = f32[4,1024]{1,0:T(4,128)} fusion(bf16[1024,2048]{1,0:T(8,128)(2,1)} %param.15, f32[4,2048]{1,0:T(4,128)S(1)} %get-tuple-element.20, f32[4,2048]{1,0:T(4,128)S(1)} %get-tuple-element.17, f32[4]{0:T(128)S(1)} %get-tuple-element.19, f32[4]{0:T(128)S(1)} %add_rsqrt_fusion.2), kind=kOutput, calls=%fused_computation.55 | convolution fusion | flops 16818176 | bytes 4276256 | tf_op jit(solution)/shard_map/dot_general | solution.py:132
  (66 shorter events, 26.8 us)
Async XLA Ops:
  0.6 13.5 %copy-start = (bf16[1024,1536]{1,0:T(8,128)(2,1)S(1)}, bf16[1024,1536]{1,0:T(8,128)(2,1)}, u32[]{:S(2)}) copy-start(bf16[1024,1536]{1,0:T(8,128)(2,1)} %param.12) | copy-start | bytes 9437188
  2.1 106.0 %all-to-all-start.4 = ((f32[32,1,4]{2,1,0:T(1,128)}), f32[32,1,4]{2,1,0:T(1,128)S(1)}, u32[]{:S(2)}, u32[]{:S(2)}) async-start(f32[32,1,4]{2,1,0:T(1,128)} %broadcast_in_dim.117), calls=%async_computation.4 | async-start | bytes 32768 | tf_op jit(solution)/shard_map/all_to_all | solution.py:16
  39.9 4.0 %copy-start.5 = (s32[1,1024]{1,0:T(1,128)S(1)}, s32[1,1024]{1,0:T(1,128)}, u32[]{:S(2)}) copy-start(s32[1,1024]{1,0:T(1,128)} %param.9) | copy-start | bytes 12292
  96.6 7.4 %copy-start.4 = (bf16[1024,1024]{0,1:T(8,128)(2,1)S(1)}, bf16[1024,1024]{0,1:T(8,128)(2,1)}, u32[]{:S(2)}) copy-start(bf16[1024,1024]{0,1:T(8,128)(2,1)} %copy.28) | copy-start | bytes 6291460
  96.6 7.4 %copy-start.9 = (bf16[512,1024]{1,0:T(8,128)(2,1)S(1)}, bf16[512,1024]{1,0:T(8,128)(2,1)}, u32[]{:S(2)}) copy-start(bf16[512,1024]{1,0:T(8,128)(2,1)} %param.13) | copy-start | bytes 3145732
  96.6 7.4 %copy-start.10 = (bf16[8,64,512]{2,1,0:T(8,128)(2,1)S(1)}, bf16[8,64,512]{2,1,0:T(8,128)(2,1)}, u32[]{:S(2)}) copy-start(bf16[8,64,512]{2,1,0:T(8,128)(2,1)} %fusion.15) | copy-start | bytes 1572868
  105.5 1.9 copy-start.3
  105.5 8.6 %copy-start.6 = (f32[1024]{0:T(1024)S(1)}, f32[1024]{0:T(1024)}, u32[]{:S(2)}) copy-start(f32[1024]{0:T(1024)} %param.14) | copy-start | bytes 12292
  108.8 9.8 %all-to-all-start.5 = ((f32[8,1,128]{2,1,0:T(1,128)}), f32[8,1,128]{2,1,0:T(1,128)S(1)}, u32[]{:S(2)}, u32[]{:S(2)}) async-start(f32[8,1,128]{2,1,0:T(1,128)} %reshape.179), calls=%async_computation.5 | async-start | bytes 8192 | tf_op jit(solution)/shard_map/all_to_all | solution.py:16
  117.0 30.3 %copy-start.8 = (s32[256]{0:T(256)S(1)}, s32[256]{0:T(256)}, u32[]{:S(2)}) copy-start(s32[256]{0:T(256)} %param.10) | copy-start | bytes 3076
  141.3 32.2 %all-to-all-start.1 = ((bf16[8,32,4,1024]{3,2,1,0:T(4,128)(2,1)}), bf16[8,32,4,1024]{3,2,1,0:T(4,128)(2,1)S(1)}, u32[]{:S(2)}, u32[]{:S(2)}) async-start(bf16[8,32,4,1024]{3,2,1,0:T(4,128)(2,1)} %broadcast_in_dim.109), calls=%async_computation.1 | async-start | bytes 4194304 | tf_op jit(solution)/shard_map/all_to_all | solution.py:16
  185.0 2.5 %copy-start.7 = (s32[4]{0:T(128)S(1)}, s32[4]{0:T(128)}, u32[]{:S(2)}) copy-start(s32[4]{0:T(128)} %param.11) | copy-start | bytes 52
  185.6 1.9 copy-start.2
  189.4 12.4 %all-to-all-start.2 = ((f32[32,1,4]{2,1,0:T(1,128)}), f32[32,1,4]{2,1,0:T(1,128)S(1)}, u32[]{:S(2)}, u32[]{:S(2)}) async-start(f32[32,1,4]{2,1,0:T(1,128)} %broadcast_in_dim.115), calls=%async_computation.2 | async-start | bytes 32768 | tf_op jit(solution)/shard_map/all_to_all | solution.py:16
  202.6 10.0 %all-to-all-start.3 = ((f32[8,1,128]{2,1,0:T(1,128)}), f32[8,1,128]{2,1,0:T(1,128)S(1)}, u32[]{:S(2)}, u32[]{:S(2)}) async-start(f32[8,1,128]{2,1,0:T(1,128)} %reshape.181), calls=%async_computation.3 | async-start | bytes 8192 | tf_op jit(solution)/shard_map/all_to_all | solution.py:16
  213.6 9.5 %copy-start.1 = (bf16[1024,1536]{1,0:T(8,128)(2,1)S(1)}, bf16[1024,1536]{1,0:T(8,128)(2,1)}, u32[]{:S(2)}) copy-start(bf16[1024,1536]{1,0:T(8,128)(2,1)} %param.12) | copy-start | bytes 9437188
where the time goes:
time: 224 us; the launch traced here: 223 us
  matrix products  65.3 us (29%)
  other arithmetic  49.8 us (22%)
  starting transfers between devices  32.5 us (15%)
  waiting for transfers between devices  31 us (14%)
  local copies, waits for them, and re-layouts  23 us (10%)
  blocking collectives  20.6 us (9%)
    sub x2, other arithmetic, attend(): exp_scores = jnp.exp(scores - row_max)  43.2 us
    all_to_all x5, starting transfers between devices, from_everyone(): return lax.all_to_all(copies, axis, split_axis=0, concat_axis=0, tiled=True)  32.5 us
    all_to_all x5, waiting for transfers between devices, from_everyone(): return lax.all_to_all(copies, axis, split_axis=0, concat_axis=0, tiled=True)  31 us
    all_to_all x1, blocking collectives, from_everyone(): return lax.all_to_all(copies, axis, split_axis=0, concat_axis=0, tiled=True)  20.6 us
    dot_general x2, matrix products, attend(): jnp.einsum('qhd,khd->hqk', query_block, keys_all, preferred_element_type=...  16.2 us
    dot_general x2, matrix products, attend(): jnp.einsum('hqk,khd->qhd', probs, values_all, preferred_element_type=jnp....  15.3 us
    dot_general x2, matrix products, embed_rows(): proj = jnp.dot(pooled, w_proj, preferred_element_type=jnp.float32)  9.4 us
    unnamed x29, local copies, waits for them, and re-layouts  9.36 us
  transfers between devices with their start and end apart: 5, of which 4 were waited for; matrix products, arithmetic and copies ran while one was open for 47% of the time, Pallas kernels for 0%

commit v1 on v0

v1 whole, which is shorter than its diff:
```python
import functools

import jax
import jax.numpy as jnp
from jax import lax
from jax.experimental import pallas as pl
from jax.experimental.pallas import tpu as pltpu
from jax.sharding import PartitionSpec as P

HEADS = 8
SCALE = 20.0
FAR = -1e30
MESH = pl.DeviceIdType.MESH
F32 = jnp.float32
BF16 = jnp.bfloat16
I32 = jnp.int32
NT = (((1,), (1,)), ((), ()))


def iota(shape, dim):
    return lax.broadcasted_iota(I32, shape, dim)


def attend_kernel(slots, seg_ref, tok_ref, wqkv_ref, wout_ref, gain_ref, pooled_ref, q_s, kt_s, v_s, qm_s, ctx_s, sum_s):
    rows, width = tok_ref.shape
    inner = wout_ref.shape[0]
    head_dim = inner // HEADS
    pairs = HEADS // 2
    tile = min(256, rows)
    qtile = 128
    seg = seg_ref[...]

    sub = iota((128, rows), 0)
    slot = sub % head_dim
    far = jnp.where(slot < slots, jnp.where(slot == seg, 0.0, FAR), 0.0)
    qm_s[...] = far.T.astype(BF16)
    half = iota((head_dim, rows), 0)
    onehot = jnp.where(half == seg, 1.0, 0.0).astype(BF16)
    for p in range(pairs):
        kt_s[2 * p, head_dim:, :] = onehot
        kt_s[2 * p + 1, :head_dim, :] = onehot

    def project(t, _):
        at = pl.ds(pl.multiple_of(t * tile, tile), tile)
        low = iota((tile, 128), 1) < head_dim
        x = tok_ref[at, :]
        qkv = jnp.dot(x, wqkv_ref[...], preferred_element_type=F32)
        q_s[at, :] = (qkv[:, :inner].astype(BF16) * head_dim**-0.5).astype(BF16)
        for p in range(pairs):
            k = qkv[:, inner + p * 128 : inner + (p + 1) * 128]
            kt = k.T.astype(BF16)
            kt_s[2 * p, :head_dim, at] = kt[:head_dim]
            kt_s[2 * p + 1, head_dim:, at] = kt[head_dim:]
            v = qkv[:, 2 * inner + p * 128 : 2 * inner + (p + 1) * 128]
            v_s[2 * p, at, :] = jnp.where(low, v, 1.0).astype(BF16)
            v_s[2 * p + 1, at, :] = jnp.where(low, 1.0, v).astype(BF16)
        return 0

    lax.fori_loop(0, rows // tile, project, 0)

    starts = [0] + [jnp.sum((seg < s).astype(F32)).astype(I32) for s in range(1, slots)] + [rows]

    def window(at, q0, first, span):
        keys = pl.ds(first, span)
        low = iota((qtile, 128), 1) < head_dim
        qm = qm_s[at, :]
        for p in range(pairs):
            q = q_s[at, p * 128 : (p + 1) * 128]
            out = []
            for h in range(2):
                qh = jnp.where(low, q, qm) if h == 0 else jnp.where(low, qm, q)
                s = jnp.dot(qh, kt_s[2 * p + h, :, keys], preferred_element_type=F32)
                e = jnp.exp(s - jnp.max(s, axis=1, keepdims=True)).astype(BF16)
                out.append(jnp.dot(e, v_s[2 * p + h, keys, :], preferred_element_type=F32))
            top = jnp.where(low, out[0], out[1])
            den = pltpu.roll(jnp.where(low, out[1], out[0]), head_dim, 1)
            ctx_s[at, p * 128 : (p + 1) * 128] = (top / den).astype(BF16)

    def queries(t, _):
        q0 = t * qtile
        at = pl.ds(pl.multiple_of(q0, qtile), qtile)
        lo = jnp.int32(0)
        hi = jnp.int32(rows)
        for s in range(1, slots):
            lo = jnp.where(starts[s] <= q0, starts[s], lo)
        for s in range(slots - 1, 0, -1):
            hi = jnp.where(starts[s] >= q0 + qtile, starts[s], hi)
        lo = lo // 128 * 128
        spans = [w for w in (512, 768) if w < rows] + [rows]
        below = jnp.int32(0)
        for w in spans:
            fits = hi - lo <= w

            @pl.when(fits & (below == 0))
            def _(w=w):
                first = 0 if w == rows else pl.multiple_of(jnp.minimum(lo, rows - w), 128)
                window(at, q0, first, w)

            below = jnp.where(fits, 1, below)
        return 0

    lax.fori_loop(0, rows // qtile, queries, 0)

    sum_s[...] = jnp.zeros_like(sum_s)

    def finish(t, _):
        at = pl.ds(pl.multiple_of(t * tile, tile), tile)
        resid = tok_ref[at, :].astype(F32) + jnp.dot(ctx_s[at, :], wout_ref[...], preferred_element_type=F32)
        centre = resid - jnp.sum(resid, axis=1, keepdims=True) * (1.0 / width)
        variance = jnp.sum(centre * centre, axis=1, keepdims=True) * (1.0 / width)
        hidden = (centre * lax.rsqrt(variance + 1e-05) * gain_ref[...]).astype(BF16)
        member = (iota((16, tile), 0) == seg_ref[:, at]).astype(F32).astype(BF16)
        sum_s[...] += jnp.dot(member, hidden, preferred_element_type=F32)
        return 0

    lax.fori_loop(0, rows // tile, finish, 0)
    sizes = jnp.sum((iota((16, rows), 0) == seg).astype(F32), axis=1, keepdims=True)
    pooled_ref[...] = (sum_s[:slots, :] / sizes[:slots]).astype(BF16)


def attend(seg, tokens, w_qkv, w_out, gain, slots):
    rows, width = tokens.shape
    inner = w_out.shape[0]
    vmem = pl.BlockSpec(memory_space=pltpu.VMEM)
    return pl.pallas_call(
        functools.partial(attend_kernel, slots),
        name="attend",
        out_shape=jax.ShapeDtypeStruct((slots, width), BF16),
        in_specs=[vmem] * 5,
        out_specs=vmem,
        scratch_shapes=[
            pltpu.VMEM((rows, inner), BF16),
            pltpu.VMEM((HEADS, 128, rows), BF16),
            pltpu.VMEM((HEADS, rows, 128), BF16),
            pltpu.VMEM((rows, 128), BF16),
            pltpu.VMEM((rows, inner), BF16),
            pltpu.VMEM((16, width), F32),
        ],
        compiler_params=pltpu.CompilerParams(vmem_limit_bytes=48 * 2**20),
    )(seg, tokens, w_qkv, w_out, gain)


def halves(x):
    hi = x.astype(BF16)
    return hi, (x - hi.astype(F32)).astype(BF16)


def loss_kernel(
    n_a, n_b, slots,
    counts_ref, pos_ref, pooled_ref, w_ref, loss_ref, grad_ref,
    colp, colm, rowg, drow, dcol, yrecv, ysend, mcol, mrow, mdr, mdc,
    p_j, g_i, unit_s, stack,
    s_colp, r_colp, s_colm, r_colm, s_row, r_row, s_dr, r_dr, s_dc, r_dc, s_y, r_y,
):
    me = lax.axis_index("dp")
    core, b, z = me % 2, (me // 2) % n_b, me // (2 * n_b)
    a = z * 2 + core
    width = pooled_ref.shape[1]
    r_rows = slots * n_b
    c_cols = slots * n_a

    def row_peer(k):
        o = (b + k) % n_b
        return o, z * (2 * n_b) + o * 2 + core

    def col_peer(k):
        o = (a + k) % n_a
        return o, (o // 2) * (2 * n_b) + b * 2 + o % 2

    barrier = pltpu.get_barrier_semaphore()

    def greet(peer):
        def step(k, _):
            pl.semaphore_signal(barrier, inc=1, device_id=(peer(k)[1],), device_id_type=MESH)
            return 0

        return step

    lax.fori_loop(1, n_b, greet(row_peer), 0)
    lax.fori_loop(1, n_a, greet(col_peer), 0)

    def exchange(peer, n, mine, source, dest, send, recv):
        def copy(k):
            o, device = peer(k)
            return pltpu.make_async_remote_copy(
                src_ref=source(o), dst_ref=dest.at[mine], send_sem=send.at[k], recv_sem=recv.at[mine],
                device_id=(device,), device_id_type=MESH,
            )

        def start():
            def step(k, _):
                copy(k).start()
                return 0

            lax.fori_loop(1, n, step, 0)

        def arrive():
            def step(k, _):
                o, device = peer(k)
                pltpu.make_async_remote_copy(
                    src_ref=source(o), dst_ref=dest.at[o], send_sem=send.at[k], recv_sem=recv.at[o],
                    device_id=(device,), device_id_type=MESH,
                ).wait_recv()
                return 0

            lax.fori_loop(1, n, step, 0)

        def drain():
            def step(k, _):
                copy(k).wait_send()
                return 0

            lax.fori_loop(1, n, step, 0)

        return start, arrive, drain

    x_colp = exchange(col_peer, n_a, a, lambda o: pooled_ref, colp, s_colp, r_colp)
    x_colm = exchange(col_peer, n_a, a, lambda o: mcol, colm, s_colm, r_colm)
    x_row = exchange(row_peer, n_b, b, lambda o: mrow, rowg, s_row, r_row)
    x_dr = exchange(row_peer, n_b, b, lambda o: mdr, drow, s_dr, r_dr)
    x_dc = exchange(col_peer, n_a, a, lambda o: mdc, dcol, s_dc, r_dc)
    x_y = exchange(row_peer, n_b, b, lambda o: ysend.at[o], yrecv, s_y, r_y)

    pl.semaphore_wait(barrier, n_a + n_b - 2)
    x_colp[0]()

    proj = jnp.dot(pooled_ref[...], w_ref[...], preferred_element_type=F32)
    rnorm = lax.rsqrt(jnp.sum(proj * proj, axis=1, keepdims=True) + 1e-06)
    unit = proj * rnorm
    unit_s[...] = unit
    s_row_id = iota((slots, 1), 0)
    mine_count = counts_ref[me]
    live_own = (s_row_id < mine_count).astype(F32)
    pos_own = jnp.zeros((slots, 1), F32)
    for s in range(slots):
        pos_own = jnp.where(s_row_id == s, pos_ref[s].astype(F32), pos_own)
    lane = iota((slots, 128), 1)
    here = lane == a * slots + iota((slots, 128), 0)
    mcol[...] = jnp.zeros_like(mcol)
    for r, value in enumerate((rnorm, pos_own, live_own)):
        mcol[r : r + 1, :] = jnp.sum(jnp.where(here, value, 0.0), axis=0, keepdims=True)
    x_colm[0]()
    g = SCALE * lax.dot_general(unit.astype(BF16), w_ref[...], NT, preferred_element_type=F32)
    mrow[:, :width] = g
    mrow[:, width:] = jnp.where(lane == 0, pos_own, jnp.where(lane == 1, live_own, 0.0))
    x_row[0]()

    colp[a] = pooled_ref[...]
    colm[a] = mcol[...]
    rowg[b] = mrow[...]
    p_j[...] = jnp.zeros_like(p_j)
    x_colp[1]()
    for o in range(n_a):
        p_j[o * slots : (o + 1) * slots, :] = colp[o].astype(F32)
    x_colm[1]()
    side = jnp.sum(colm[...], axis=0)
    rnorm_j, pos_j, live_j = side[0:1], side[1:2], side[2:3] > 0.5
    x_row[1]()
    for o in range(n_b):
        g_i[o * slots : (o + 1) * slots, :] = rowg[o]

    p_b = p_j[...].astype(BF16)
    g_hi, g_lo = halves(g_i[:, :width])
    tail = g_i[:, width:]
    pos_i, live_i = tail[:, 0:1], tail[:, 1:2] > 0.5
    logits = lax.dot_general(g_hi, p_b, NT, preferred_element_type=F32)
    logits += lax.dot_general(g_lo, p_b, NT, preferred_element_type=F32)
    logits = logits * rnorm_j
    r = iota((r_rows, 128), 0)
    c = iota((r_rows, 128), 1)
    id_i = (z * (2 * n_b) + (r // slots) * 2 + core) * slots + r % slots
    o_j = c // slots
    id_j = ((o_j // 2) * (2 * n_b) + b * 2 + o_j % 2) * slots + c % slots
    eye = r == c
    inside = (c < c_cols) & (id_i != id_j)
    expd = jnp.exp(jnp.where(c < c_cols, logits, 0.0))
    exp_i = jnp.where(inside & live_j, expd, 0.0)
    exp_j = jnp.where(inside & live_i, expd, 0.0)
    hit_i = (pos_i == id_j.astype(F32)) & (c < c_cols)
    hit_j = (pos_j == id_i.astype(F32)) & (c < c_cols)
    part_i = jnp.sum(exp_i, axis=1, keepdims=True)
    picked = jnp.sum(jnp.where(hit_i, logits, 0.0), axis=1, keepdims=True)
    mdr[...] = jnp.zeros_like(mdr)
    mdr[0:1, :] = jnp.sum(jnp.where(eye, part_i, 0.0), axis=0, keepdims=True)
    mdr[1:2, :] = jnp.sum(jnp.where(eye, picked, 0.0), axis=0, keepdims=True)
    mdc[...] = jnp.zeros_like(mdc)
    mdc[0:1, :] = jnp.sum(exp_j, axis=0, keepdims=True)
    x_dr[0]()
    x_dc[0]()
    drow[b] = mdr[...]
    dcol[a] = mdc[...]
    x_dr[1]()
    x_dc[1]()
    side_i = jnp.sum(drow[...], axis=0)
    den_j = jnp.sum(dcol[...], axis=0)[0:1]
    den_i = jnp.sum(jnp.where(eye, side_i[0:1], 0.0), axis=1, keepdims=True)
    w_i = jnp.where(live_i, exp_i / den_i - hit_i.astype(F32), 0.0).astype(BF16).astype(F32)
    den_j = jnp.where(den_j > 0.0, den_j, 1.0)
    w_j = jnp.where(live_j & (c < c_cols), exp_j / den_j - hit_j.astype(F32), 0.0).astype(BF16).astype(F32)
    mix_hi, mix_lo = halves((w_i + w_j) * rnorm_j)
    y = jnp.dot(mix_hi, p_b, preferred_element_type=F32) + jnp.dot(mix_lo, p_b, preferred_element_type=F32)
    for o in range(n_b):
        ysend[o] = y[o * slots : (o + 1) * slots]
    x_y[0]()
    yrecv[b] = ysend[b]

    table = jnp.log(side_i[0:1]) - side_i[1:2]
    mine = jnp.sum(jnp.where(lane == b * slots + iota((slots, 128), 0), table, 0.0), axis=1, keepdims=True)
    mine = jnp.where(live_own > 0.5, mine, 0.0)
    loss_lane = jnp.sum(jnp.where(lane == iota((slots, 128), 0), mine, 0.0), axis=0, keepdims=True)
    loss_ref[...] = loss_lane[:, :slots]

    x_y[1]()
    y_own = jnp.sum(yrecv[...], axis=0)
    y_hi = y_own.astype(BF16).astype(F32)
    stack[:slots, :] = y_hi
    stack[slots:, :] = y_own - y_hi
    d = jnp.dot(stack[...].astype(BF16), w_ref[...], preferred_element_type=F32)
    d_emb = SCALE * (d[:slots] + d[slots:])
    own = unit_s[...]
    radial = jnp.sum(d_emb * own, axis=1, keepdims=True)
    d_proj = ((d_emb - radial * own) * rnorm).astype(BF16)
    grad_ref[...] = lax.dot_general(d_proj, w_ref[...], NT, preferred_element_type=F32)
    for x in (x_colp, x_colm, x_row, x_dr, x_dc, x_y):
        x[2]()


def contrast(counts, positives, pooled, w_proj, n_a, n_b):
    slots, width = pooled.shape
    embed = w_proj.shape[1]
    vmem = pl.BlockSpec(memory_space=pltpu.VMEM)
    smem = pl.BlockSpec(memory_space=pltpu.SMEM)
    sems = [pltpu.SemaphoreType.DMA((n,)) for n in (n_a, n_a, n_a, n_a, n_b, n_b, n_b, n_b, n_a, n_a, n_b, n_b)]
    return pl.pallas_call(
        functools.partial(loss_kernel, n_a, n_b, slots),
        name="contrast",
        out_shape=(jax.ShapeDtypeStruct((1, slots), F32), jax.ShapeDtypeStruct((slots, width), F32)),
        in_specs=[smem, smem, vmem, vmem],
        out_specs=(vmem, vmem),
        scratch_shapes=[
            pltpu.VMEM((n_a, slots, width), BF16),
            pltpu.VMEM((n_a, 8, 128), F32),
            pltpu.VMEM((n_b, slots, width + 128), F32),
            pltpu.VMEM((n_b, 8, 128), F32),
            pltpu.VMEM((n_a, 8, 128), F32),
            pltpu.VMEM((n_b, slots, width), F32),
            pltpu.VMEM((n_b, slots, width), F32),
            pltpu.VMEM((8, 128), F32),
            pltpu.VMEM((slots, width + 128), F32),
            pltpu.VMEM((8, 128), F32),
            pltpu.VMEM((8, 128), F32),
            pltpu.VMEM((128, width), F32),
            pltpu.VMEM((slots * n_b, width + 128), F32),
            pltpu.VMEM((slots, embed), F32),
            pltpu.VMEM((2 * slots, width), F32),
            *sems,
        ],
        compiler_params=pltpu.CompilerParams(collective_id=0, has_side_effects=True, vmem_limit_bytes=32 * 2**20),
    )(counts, positives, pooled, w_proj)


def body(n_a, n_b, tokens, seg_ids, counts, positives, w_qkv, w_out, ln_gain, w_proj):
    slots = positives.shape[0]
    pooled = attend(seg_ids, tokens, w_qkv, w_out, ln_gain[None, :], slots)
    loss, grad = contrast(counts, positives, pooled, w_proj, n_a, n_b)
    return loss.reshape(slots), grad


def solution(mesh):
    n_b = 16
    n_a = mesh.size // n_b
    return jax.shard_map(
        functools.partial(body, n_a, n_b),
        mesh=mesh,
        in_specs=(P("dp", None), P("dp", None), P(), P("dp"), P(), P(), P(), P()),
        out_specs=(P("dp"), P("dp", None)),
        check_vma=False,
    )
```

time: 224 us -> 70.2 us (0.31)
  matrix products: 65.3 us -> 0 us
  Pallas kernels: 0 us -> 63.9 us
  other arithmetic: 49.8 us -> 0 us
  starting transfers between devices: 32.5 us -> 0 us
  waiting for transfers between devices: 31 us -> 0 us
  blocking collectives: 20.6 us -> 0 us
  local copies, waits for them, and re-layouts: 23 us -> 5.31 us
    dot_general x13 -> x0, matrix products: 65.3 us -> none  [the longest x2 16.2 us: attend(): jnp.einsum('qhd,khd->hqk', query_block, keys_all, preferred_element_type=...]
    pallas_call x0 -> x2, Pallas kernels: none -> 63.9 us  [the longest x1 35.7 us: contrast(): pl.pallas_call(functools.partial(loss_kernel, n_a, n_b, slots), name='con...]
    sub x2 -> x0, other arithmetic: 43.2 us -> none  [attend(): exp_scores = jnp.exp(scores - row_max)]
    all_to_all x5 -> x0, starting transfers between devices: 32.5 us -> none  [from_everyone(): return lax.all_to_all(copies, axis, split_axis=0, concat_axis=0, tiled=True)]
    all_to_all x5 -> x0, waiting for transfers between devices: 31 us -> none  [from_everyone(): return lax.all_to_all(copies, axis, split_axis=0, concat_axis=0, tiled=True)]
    all_to_all x1 -> x0, blocking collectives: 20.6 us -> none  [from_everyone(): return lax.all_to_all(copies, axis, split_axis=0, concat_axis=0, tiled=True)]
    unnamed x29 -> x16, local copies, waits for them, and re-layouts: 9.36 us -> 5.31 us
    broadcast_in_dim x5 -> x0, local copies, waits for them, and re-layouts: 3.47 us -> none  [the longest x4 3.38 us: from_everyone(): copies = jnp.broadcast_to(shard, (lax.axis_size(axis), *shard.shape))]
  transfers between devices with their start and end apart: 5 -> 0, of which waited for: 4 -> 0; matrix products, arithmetic and copies ran while one was open for 47% -> 0% of each run, Pallas kernels for 0% -> 0%
where the time goes in v1:
time: 70.2 us; the launch traced here: 69.9 us
  Pallas kernels  63.9 us (91%)
  local copies, waits for them, and re-layouts  5.31 us (8%)
    pallas_call x1, Pallas kernels, contrast(): pl.pallas_call(functools.partial(loss_kernel, n_a, n_b, slots), name='con...  35.7 us
    pallas_call x1, Pallas kernels, attend(): pl.pallas_call(functools.partial(attend_kernel, slots), name='attend', ou...  28.2 us
    unnamed x16, local copies, waits for them, and re-layouts  5.31 us

profile of v1, /device:TPU:1, one launch (start us, length us, event | category | flops | bytes accessed | tf_op | source)
XLA Modules:
  0.0 69.9 jit_solution(2445749517110820007)
XLA Ops:
  0.6 0.0 copy-start.1
  0.6 1.6 %copy-done.1 = bf16[1024,1024]{1,0:T(8,128)(2,1)S(1)} copy-done((bf16[1024,1024]{1,0:T(8,128)(2,1)S(1)}, bf16[1024,1024]{1,0:T(8,128)(2,1)}, u32[]{:S(2)}) %copy-start.1) | copy-done | bytes 2097176
  2.2 0.0 copy-start.2
  2.2 1.2 %copy-done.2 = bf16[512,1024]{1,0:T(8,128)(2,1)S(1)} copy-done((bf16[512,1024]{1,0:T(8,128)(2,1)S(1)}, bf16[512,1024]{1,0:T(8,128)(2,1)}, u32[]{:S(2)}) %copy-start.2) | copy-done | bytes 1048600
  3.5 0.0 copy-start.3
  3.5 0.7 copy-done.3
  4.1 0.0 copy-start.4
  4.1 0.7 copy-done.4
  4.8 0.0 copy-start
  4.8 0.0 copy-start.5
  4.8 0.0 copy-start.6
  4.8 28.2 %attend.1.pooled_ref = bf16[4,1024]{1,0:T(4,128)(2,1)S(1)} custom-call(s32[1,1024]{1,0:T(1,128)S(1)} %copy-done.3, bf16[1024,1024]{1,0:T(8,128)(2,1)S(1)} %copy-done.1, bf16[1024,1536]{1,0:T(8,128)(2,1)} %wqkv_ref.1, bf16[512,1024]{1,0:T(8,128)(2,1)S(1)} %copy-done.2, f32[1,1024]{1,0:T(1,128)S(1)} %bitcast.2), custom_call_target="tpu_custom_call" | custom-call | tf_op jit(solution)/shard_map/attend/pallas_call | solution.py:125
  33.0 0.0 copy-done
  33.0 0.0 copy-done.5
  33.0 0.0 copy-done.6
  33.1 35.7 %contrast.1 = (f32[1,4]{1,0:T(1,128)S(1)}, f32[4,1024]{1,0:T(4,128)S(1)}) custom-call(s32[256]{0:T(256)S(1)} %copy-done.5, s32[4]{0:T(128)S(1)} %copy-done.6, bf16[4,1024]{1,0:T(4,128)(2,1)S(1)} %attend.1.pooled_ref, bf16[1024,2048]{1,0:T(8,128)(2,1)S(1)} %copy-done), custom_call_target="tpu_custom_call" | custom-call | tf_op jit(solution)/shard_map/contrast/pallas_call | solution.py:334
  68.8 0.5 copy.12
  69.3 0.6 copy.13
Async XLA Ops:
  0.6 1.6 %copy-start.1 = (bf16[1024,1024]{1,0:T(8,128)(2,1)S(1)}, bf16[1024,1024]{1,0:T(8,128)(2,1)}, u32[]{:S(2)}) copy-start(bf16[1024,1024]{1,0:T(8,128)(2,1)} %tok_ref.1) | copy-start | bytes 6291460
  2.2 1.2 %copy-start.2 = (bf16[512,1024]{1,0:T(8,128)(2,1)S(1)}, bf16[512,1024]{1,0:T(8,128)(2,1)}, u32[]{:S(2)}) copy-start(bf16[512,1024]{1,0:T(8,128)(2,1)} %wout_ref.1) | copy-start | bytes 3145732
  3.5 0.7 copy-start.3
  4.1 0.7 copy-start.4
  4.8 28.2 %copy-start = (bf16[1024,2048]{1,0:T(8,128)(2,1)S(1)}, bf16[1024,2048]{1,0:T(8,128)(2,1)}, u32[]{:S(2)}) copy-start(bf16[1024,2048]{1,0:T(8,128)(2,1)} %w_ref.1) | copy-start | bytes 12582916
  4.8 28.2 %copy-start.5 = (s32[256]{0:T(256)S(1)}, s32[256]{0:T(256)}, u32[]{:S(2)}) copy-start(s32[256]{0:T(256)} %counts_ref.1) | copy-start | bytes 3076
  4.8 28.2 %copy-start.6 = (s32[4]{0:T(128)S(1)}, s32[4]{0:T(128)}, u32[]{:S(2)}) copy-start(s32[4]{0:T(128)} %pos_ref.1) | copy-start | bytes 52

commit v2 on v1

v2 whole, which is shorter than its diff:
```python
import functools

import jax
import jax.numpy as jnp
from jax import lax
from jax.experimental import pallas as pl
from jax.experimental.pallas import tpu as pltpu
from jax.sharding import PartitionSpec as P

HEADS = 8
SCALE = 20.0
FAR = -1e30
MESH = pl.DeviceIdType.MESH
F32 = jnp.float32
BF16 = jnp.bfloat16
I32 = jnp.int32
NT = (((1,), (1,)), ((), ()))


def iota(shape, dim):
    return lax.broadcasted_iota(I32, shape, dim)


def attend_kernel(slots, seg_ref, tok_hbm, wqkv_hbm, ctx_ref, tok_ref, wqkv_ref, q_s, kt_s, v_s, qm_s, sem):
    rows = tok_ref.shape[0]
    inner = ctx_ref.shape[1]
    head_dim = inner // HEADS
    pairs = HEADS // 2
    tile = min(256, rows)
    qtile = 128

    w_copy = pltpu.make_async_copy(wqkv_hbm, wqkv_ref, sem.at[0])
    w_copy.start()

    def tok_copy(t):
        at = pl.ds(pl.multiple_of(t * tile, tile), tile)
        return pltpu.make_async_copy(tok_hbm.at[at, :], tok_ref.at[at, :], sem.at[t + 1])

    for t in range(rows // tile):
        tok_copy(t).start()
    seg = seg_ref[...]

    sub = iota((128, rows), 0)
    slot = sub % head_dim
    far = jnp.where(slot < slots, jnp.where(slot == seg, 0.0, FAR), 0.0)
    qm_s[...] = far.T.astype(BF16)
    half = iota((head_dim, rows), 0)
    onehot = jnp.where(half == seg, 1.0, 0.0).astype(BF16)
    for p in range(pairs):
        kt_s[2 * p, head_dim:, :] = onehot
        kt_s[2 * p + 1, :head_dim, :] = onehot

    starts = [0] + [jnp.sum((seg < s).astype(F32)).astype(I32) for s in range(1, slots)] + [rows]

    w_copy.wait()

    def project(t, _):
        tok_copy(t).wait()
        at = pl.ds(pl.multiple_of(t * tile, tile), tile)
        low = iota((tile, 128), 1) < head_dim
        x = tok_ref[at, :]
        qkv = jnp.dot(x, wqkv_ref[...], preferred_element_type=F32)
        q_s[at, :] = (qkv[:, :inner].astype(BF16) * head_dim**-0.5).astype(BF16)
        for p in range(pairs):
            k = qkv[:, inner + p * 128 : inner + (p + 1) * 128]
            kt = k.T.astype(BF16)
            kt_s[2 * p, :head_dim, at] = kt[:head_dim]
            kt_s[2 * p + 1, head_dim:, at] = kt[head_dim:]
            v = qkv[:, 2 * inner + p * 128 : 2 * inner + (p + 1) * 128]
            v_s[2 * p, at, :] = jnp.where(low, v, 1.0).astype(BF16)
            v_s[2 * p + 1, at, :] = jnp.where(low, 1.0, v).astype(BF16)
        return 0

    lax.fori_loop(0, rows // tile, project, 0)

    def window(at, first, span):
        keys = pl.ds(first, span)
        low = iota((qtile, 128), 1) < head_dim
        qm = qm_s[at, :]
        scores = []
        for n in range(HEADS):
            q = q_s[at, n // 2 * 128 : (n // 2 + 1) * 128]
            q = jnp.where(low, q, qm) if n % 2 == 0 else jnp.where(low, qm, q)
            scores.append(jnp.dot(q, kt_s[n, :, keys], preferred_element_type=F32))
        exps = [jnp.exp(s - jnp.max(s, axis=1, keepdims=True)).astype(BF16) for s in scores]
        outs = [jnp.dot(e, v_s[n, keys, :], preferred_element_type=F32) for n, e in enumerate(exps)]
        for p in range(pairs):
            top = jnp.where(low, outs[2 * p], outs[2 * p + 1])
            den = pltpu.roll(jnp.where(low, outs[2 * p + 1], outs[2 * p]), head_dim, 1)
            ctx_ref[at, p * 128 : (p + 1) * 128] = (top / den).astype(BF16)

    def queries(t, _):
        q0 = t * qtile
        at = pl.ds(pl.multiple_of(q0, qtile), qtile)
        lo = jnp.int32(0)
        hi = jnp.int32(rows)
        for s in range(1, slots):
            lo = jnp.where(starts[s] <= q0, starts[s], lo)
        for s in range(slots - 1, 0, -1):
            hi = jnp.where(starts[s] >= q0 + qtile, starts[s], hi)
        lo = lo // 128 * 128
        spans = [w for w in (512, 768) if w < rows] + [rows]
        below = jnp.int32(0)
        for w in spans:
            fits = hi - lo <= w

            @pl.when(fits & (below == 0))
            def _(w=w):
                first = 0 if w == rows else pl.multiple_of(jnp.minimum(lo, rows - w), 128)
                window(at, first, w)

            below = jnp.where(fits, 1, below)
        return 0

    lax.fori_loop(0, rows // qtile, queries, 0)


def attend(seg, tokens, w_qkv, slots):
    rows, width = tokens.shape
    inner = w_qkv.shape[1] // 3
    vmem = pl.BlockSpec(memory_space=pltpu.VMEM)
    hbm = pl.BlockSpec(memory_space=pltpu.HBM)
    return pl.pallas_call(
        functools.partial(attend_kernel, slots),
        name="attend",
        out_shape=jax.ShapeDtypeStruct((rows, inner), BF16),
        in_specs=[vmem, hbm, hbm],
        out_specs=vmem,
        scratch_shapes=[
            pltpu.VMEM((rows, width), BF16),
            pltpu.VMEM((width, 3 * inner), BF16),
            pltpu.VMEM((rows, inner), BF16),
            pltpu.VMEM((HEADS, 128, rows), BF16),
            pltpu.VMEM((HEADS, rows, 128), BF16),
            pltpu.VMEM((rows, 128), BF16),
            pltpu.SemaphoreType.DMA((1 + rows // min(256, rows),)),
        ],
        compiler_params=pltpu.CompilerParams(vmem_limit_bytes=40 * 2**20),
        cost_estimate=pl.CostEstimate(flops=8 * 10**9, bytes_accessed=6 * 2**20, transcendentals=4 * 10**6),
    )(seg, tokens, w_qkv)


def halves(x):
    hi = x.astype(BF16)
    return hi, (x - hi.astype(F32)).astype(BF16)


def loss_kernel(
    n_a, n_b, slots,
    counts_ref, pos_ref, seg_ref, tok_ref, ctx_ref, wout_ref, gain_ref, w_ref, loss_ref, grad_ref,
    mine_s, colp, rowp, colm, rowm, drow, dcol, yrecv, ysend, mcol, mrow, mdr, mdc,
    sum_s, p_s, unit_s, emb_s, wt_s, stack,
    s_colp, r_colp, s_rowp, r_rowp, s_colm, r_colm, s_rowm, r_rowm, s_dr, r_dr, s_dc, r_dc, s_y, r_y,
):
    me = lax.axis_index("dp")
    core, b, z = me % 2, (me // 2) % n_b, me // (2 * n_b)
    a = z * 2 + core
    rows, width = tok_ref.shape
    embed = w_ref.shape[1]
    r_rows = slots * n_b
    c_cols = slots * n_a

    def row_peer(k):
        o = (b + k) % n_b
        return o, z * (2 * n_b) + o * 2 + core

    def col_peer(k):
        o = (a + k) % n_a
        return o, (o // 2) * (2 * n_b) + b * 2 + o % 2

    barrier = pltpu.get_barrier_semaphore()

    def greet(peer):
        def step(k, _):
            pl.semaphore_signal(barrier, inc=1, device_id=(peer(k)[1],), device_id_type=MESH)
            return 0

        return step

    lax.fori_loop(1, n_b, greet(row_peer), 0)
    lax.fori_loop(1, n_a, greet(col_peer), 0)

    def exchange(peer, n, mine, source, dest, send, recv):
        def copy(k):
            o, device = peer(k)
            return pltpu.make_async_remote_copy(
                src_ref=source(o), dst_ref=dest.at[mine], send_sem=send.at[k], recv_sem=recv.at[mine],
                device_id=(device,), device_id_type=MESH,
            )

        def start():
            def step(k, _):
                copy(k).start()
                return 0

            lax.fori_loop(1, n, step, 0)

        def arrive():
            def step(k, _):
                o, device = peer(k)
                pltpu.make_async_remote_copy(
                    src_ref=source(o), dst_ref=dest.at[o], send_sem=send.at[k], recv_sem=recv.at[o],
                    device_id=(device,), device_id_type=MESH,
                ).wait_recv()
                return 0

            lax.fori_loop(1, n, step, 0)

        def drain():
            def step(k, _):
                copy(k).wait_send()
                return 0

            lax.fori_loop(1, n, step, 0)

        return start, arrive, drain

    x_colp = exchange(col_peer, n_a, a, lambda o: mine_s, colp, s_colp, r_colp)
    x_rowp = exchange(row_peer, n_b, b, lambda o: mine_s, rowp, s_rowp, r_rowp)
    x_colm = exchange(col_peer, n_a, a, lambda o: mcol, colm, s_colm, r_colm)
    x_rowm = exchange(row_peer, n_b, b, lambda o: mrow, rowm, s_rowm, r_rowm)
    x_dr = exchange(row_peer, n_b, b, lambda o: mdr, drow, s_dr, r_dr)
    x_dc = exchange(col_peer, n_a, a, lambda o: mdc, dcol, s_dc, r_dc)
    x_y = exchange(row_peer, n_b, b, lambda o: ysend.at[o], yrecv, s_y, r_y)

    s_id = iota((slots, 1), 0)
    lane = iota((slots, 128), 1)
    live_own = (s_id < counts_ref[me]).astype(F32)
    pos_own = jnp.zeros((slots, 1), F32)
    for s in range(slots):
        pos_own = jnp.where(s_id == s, pos_ref[s].astype(F32), pos_own)
    for ref, first in ((mcol, a * slots), (mrow, b * slots)):
        here = lane == first + iota((slots, 128), 0)
        ref[0:1, :] = jnp.sum(jnp.where(here, pos_own, 0.0), axis=0, keepdims=True)
        ref[1:2, :] = jnp.sum(jnp.where(here, live_own, 0.0), axis=0, keepdims=True)

    tile = min(256, rows)
    sum_s[...] = jnp.zeros_like(sum_s)

    def finish(t, _):
        at = pl.ds(pl.multiple_of(t * tile, tile), tile)
        resid = tok_ref[at, :].astype(F32) + jnp.dot(ctx_ref[at, :], wout_ref[...], preferred_element_type=F32)
        centre = resid - jnp.sum(resid, axis=1, keepdims=True) * (1.0 / width)
        variance = jnp.sum(centre * centre, axis=1, keepdims=True) * (1.0 / width)
        hidden = (centre * lax.rsqrt(variance + 1e-05) * gain_ref[...]).astype(BF16)
        member = (iota((16, tile), 0) == seg_ref[:, at]).astype(F32).astype(BF16)
        sum_s[...] += jnp.dot(member, hidden, preferred_element_type=F32)
        return 0

    lax.fori_loop(0, rows // tile, finish, 0)
    sizes = jnp.sum((iota((16, rows), 0) == seg_ref[...]).astype(F32), axis=1, keepdims=True)
    pooled = (sum_s[:slots, :] / sizes[:slots]).astype(BF16)
    mine_s[...] = pooled

    pl.semaphore_wait(barrier, n_a + n_b - 2)
    x_colm[0]()
    x_rowm[0]()
    x_colp[0]()
    x_rowp[0]()

    proj = jnp.dot(pooled, w_ref[...], preferred_element_type=F32)
    rnorm = lax.rsqrt(jnp.sum(proj * proj, axis=1, keepdims=True) + 1e-06)
    unit_s[...] = proj * rnorm

    def turn(j, _):
        at = pl.ds(pl.multiple_of(j * 128, 128), 128)
        wt_s[at, :] = w_ref[:, at].T
        return 0

    lax.fori_loop(0, embed // 128, turn, 0)
    colp[a] = pooled
    rowp[b] = pooled
    colm[a] = mcol[...]
    rowm[b] = mrow[...]
    p_s[...] = jnp.zeros_like(p_s)
    x_colm[1]()
    x_rowm[1]()
    x_colp[1]()
    for o in range(n_a):
        p_s[o * slots : (o + 1) * slots, :] = colp[o].astype(F32)
    x_rowp[1]()
    for o in range(n_b):
        p_s[128 + o * slots : 128 + (o + 1) * slots, :] = rowp[o].astype(F32)

    p_b = p_s[...].astype(BF16)
    proj_all = jnp.dot(p_b, w_ref[...], preferred_element_type=F32)
    rnorm_all = lax.rsqrt(jnp.sum(proj_all * proj_all, axis=1, keepdims=True) + 1e-06)
    emb_s[...] = (proj_all * rnorm_all).astype(BF16)
    logits = SCALE * lax.dot_general(emb_s[128 : 128 + r_rows, :], emb_s[:128, :], NT, preferred_element_type=F32)

    r = iota((r_rows, 128), 0)
    c = iota((r_rows, 128), 1)
    id_i = (z * (2 * n_b) + (r // slots) * 2 + core) * slots + r % slots
    o_j = c // slots
    id_j = ((o_j // 2) * (2 * n_b) + b * 2 + o_j % 2) * slots + c % slots
    eye = r == c
    square = iota((128, 128), 0) == iota((128, 128), 1)
    rnorm_j = jnp.sum(jnp.where(square, rnorm_all[:128], 0.0), axis=0, keepdims=True)
    side_j = jnp.sum(colm[...], axis=0)
    side_i = jnp.sum(rowm[...], axis=0)
    pos_j, live_j = side_j[0:1], side_j[1:2] > 0.5
    pos_i = jnp.sum(jnp.where(eye, side_i[0:1], 0.0), axis=1, keepdims=True)
    live_i = jnp.sum(jnp.where(eye, side_i[1:2], 0.0), axis=1, keepdims=True) > 0.5
    inside = (c < c_cols) & (id_i != id_j)
    expd = jnp.exp(logits)
    exp_i = jnp.where(inside & live_j, expd, 0.0)
    exp_j = jnp.where(inside & live_i, expd, 0.0)
    hit_i = (pos_i == id_j.astype(F32)) & (c < c_cols)
    hit_j = (pos_j == id_i.astype(F32)) & (c < c_cols)
    part_i = jnp.sum(exp_i, axis=1, keepdims=True)
    picked = jnp.sum(jnp.where(hit_i, logits, 0.0), axis=1, keepdims=True)
    mdc[...] = jnp.sum(exp_j, axis=0, keepdims=True)
    mdr[0:1, :] = jnp.sum(jnp.where(eye, part_i, 0.0), axis=0, keepdims=True)
    mdr[1:2, :] = jnp.sum(jnp.where(eye, picked, 0.0), axis=0, keepdims=True)
    x_dc[0]()
    x_dr[0]()
    drow[b] = mdr[...]
    dcol[a] = mdc[...]
    x_dr[1]()
    x_dc[1]()
    sums_i = jnp.sum(drow[...], axis=0)
    den_j = jnp.sum(dcol[...], axis=0)
    den_i = jnp.sum(jnp.where(eye, sums_i[0:1], 0.0), axis=1, keepdims=True)
    w_i = jnp.where(live_i, exp_i / den_i - hit_i.astype(F32), 0.0)
    den_j = jnp.where(den_j > 0.0, den_j, 1.0)
    w_j = jnp.where(live_j & (c < c_cols), exp_j / den_j - hit_j.astype(F32), 0.0)
    mix_hi, mix_lo = halves((w_i + w_j) * rnorm_j)
    p_j = p_b[:128]
    y = jnp.dot(mix_hi, p_j, preferred_element_type=F32) + jnp.dot(mix_lo, p_j, preferred_element_type=F32)
    for o in range(n_b):
        ysend[o] = y[o * slots : (o + 1) * slots]
    x_y[0]()
    yrecv[b] = ysend[b]

    table = jnp.log(sums_i[0:1]) - sums_i[1:2]
    mine = jnp.sum(jnp.where(lane == b * slots + iota((slots, 128), 0), table, 0.0), axis=1, keepdims=True)
    mine = jnp.where(live_own > 0.5, mine, 0.0)
    loss_lane = jnp.sum(jnp.where(lane == iota((slots, 128), 0), mine, 0.0), axis=0, keepdims=True)
    loss_ref[...] = loss_lane[:, :slots]

    x_y[1]()
    y_own = jnp.sum(yrecv[...], axis=0)
    y_hi = y_own.astype(BF16).astype(F32)
    stack[:slots, :] = y_hi
    stack[slots:, :] = y_own - y_hi
    d = jnp.dot(stack[...].astype(BF16), w_ref[...], preferred_element_type=F32)
    d_emb = SCALE * (d[:slots] + d[slots:])
    own = unit_s[...]
    radial = jnp.sum(d_emb * own, axis=1, keepdims=True)
    d_proj = ((d_emb - radial * own) * rnorm).astype(BF16)
    grad_ref[...] = jnp.dot(d_proj, wt_s[...], preferred_element_type=F32)
    for x in (x_colm, x_rowm, x_colp, x_rowp, x_dr, x_dc, x_y):
        x[2]()


def contrast(counts, positives, seg, tokens, ctx, w_out, gain, w_proj, n_a, n_b):
    slots = positives.shape[0]
    width, embed = w_proj.shape
    vmem = pl.BlockSpec(memory_space=pltpu.VMEM)
    smem = pl.BlockSpec(memory_space=pltpu.SMEM)
    sems = [pltpu.SemaphoreType.DMA((n,)) for n in (n_a, n_b, n_a, n_b, n_b, n_a, n_b) for _ in range(2)]
    return pl.pallas_call(
        functools.partial(loss_kernel, n_a, n_b, slots),
        name="contrast",
        out_shape=(jax.ShapeDtypeStruct((1, slots), F32), jax.ShapeDtypeStruct((slots, width), F32)),
        in_specs=[smem, smem] + [vmem] * 6,
        out_specs=(vmem, vmem),
        scratch_shapes=[
            pltpu.VMEM((slots, width), BF16),
            pltpu.VMEM((n_a, slots, width), BF16),
            pltpu.VMEM((n_b, slots, width), BF16),
            pltpu.VMEM((n_a, 2, 128), F32),
            pltpu.VMEM((n_b, 2, 128), F32),
            pltpu.VMEM((n_b, 2, 128), F32),
            pltpu.VMEM((n_a, 1, 128), F32),
            pltpu.VMEM((n_b, slots, width), F32),
            pltpu.VMEM((n_b, slots, width), F32),
            pltpu.VMEM((2, 128), F32),
            pltpu.VMEM((2, 128), F32),
            pltpu.VMEM((2, 128), F32),
            pltpu.VMEM((1, 128), F32),
            pltpu.VMEM((16, width), F32),
            pltpu.VMEM((128 + slots * n_b, width), F32),
            pltpu.VMEM((slots, embed), F32),
            pltpu.VMEM((128 + slots * n_b, embed), BF16),
            pltpu.VMEM((embed, width), BF16),
            pltpu.VMEM((2 * slots, width), F32),
            *sems,
        ],
        compiler_params=pltpu.CompilerParams(collective_id=0, has_side_effects=True, vmem_limit_bytes=40 * 2**20),
    )(counts, positives, seg, tokens, ctx, w_out, gain, w_proj)


def body(n_a, n_b, tokens, seg_ids, counts, positives, w_qkv, w_out, ln_gain, w_proj):
    slots = positives.shape[0]
    ctx = attend(seg_ids, tokens, w_qkv, slots)
    loss, grad = contrast(counts, positives, seg_ids, tokens, ctx, w_out, ln_gain[None, :], w_proj, n_a, n_b)
    return loss.reshape(slots), grad


def solution(mesh):
    n_b = 16
    n_a = mesh.size // n_b
    return jax.shard_map(
        functools.partial(body, n_a, n_b),
        mesh=mesh,
        in_specs=(P("dp", None), P("dp", None), P(), P("dp"), P(), P(), P(), P()),
        out_specs=(P("dp"), P("dp", None)),
        check_vma=False,
    )
```

time: 70.2 us -> 52 us (0.74)
  Pallas kernels: 63.9 us -> 45.7 us
    pallas_call x1, Pallas kernels: 28.2 us -> 11.7 us  [attend(): pl.pallas_call(functools.partial(attend_kernel, slots), name='attend', ou...]
    pallas_call x1, Pallas kernels: 35.7 us -> 34.1 us  [contrast(): pl.pallas_call(functools.partial(loss_kernel, n_a, n_b, slots), name='con...]
    unnamed x16 -> x18, local copies, waits for them, and re-layouts: 5.31 us -> 5.3 us
where the time goes in v2:
time: 52 us; the launch traced here: 51.7 us
  Pallas kernels  45.7 us (88%)
  local copies, waits for them, and re-layouts  5.3 us (10%)
  between operations  0.71 us (1%)
    pallas_call x1, Pallas kernels, contrast(): pl.pallas_call(functools.partial(loss_kernel, n_a, n_b, slots), name='con...  34.1 us
    pallas_call x1, Pallas kernels, attend(): pl.pallas_call(functools.partial(attend_kernel, slots), name='attend', ou...  11.7 us
    unnamed x18, local copies, waits for them, and re-layouts  5.3 us

profile of v2, /device:TPU:1, one launch (start us, length us, event | category | flops | bytes accessed | tf_op | source)
XLA Modules:
  0.0 51.7 jit_solution(9519184473571353256)
XLA Ops:
  0.6 0.0 copy-start.1
  0.6 1.6 %copy-done.1 = bf16[1024,1024]{1,0:T(8,128)(2,1)S(1)} copy-done((bf16[1024,1024]{1,0:T(8,128)(2,1)S(1)}, bf16[1024,1024]{1,0:T(8,128)(2,1)}, u32[]{:S(2)}) %copy-start.1) | copy-done | bytes 2097176
  2.2 0.0 copy-start.3
  2.2 0.7 %copy-done.3 = s32[1,1024]{1,0:T(1,128)S(1)} copy-done((s32[1,1024]{1,0:T(1,128)S(1)}, s32[1,1024]{1,0:T(1,128)}, u32[]{:S(2)}) %copy-start.3) | copy-done | bytes 4120
  2.9 0.0 copy-start.7
  2.9 1.9 %copy-done.7 = bf16[1024,1536]{1,0:T(8,128)(2,1)S(1)} copy-done((bf16[1024,1536]{1,0:T(8,128)(2,1)S(1)}, bf16[1024,1536]{1,0:T(8,128)(2,1)}, u32[]{:S(2)}) %copy-start.7) | copy-done | bytes 3145752
  4.8 0.0 copy-start
  4.8 0.0 copy-start.2
  4.8 0.0 copy-start.4
  4.8 0.0 copy-start.5
  4.8 0.0 copy-start.6
  4.8 11.7 %attend.1.ctx_ref = bf16[1024,512]{1,0:T(8,128)(2,1)S(1)} custom-call(s32[1,1024]{1,0:T(1,128)S(1)} %copy-done.3, bf16[1024,1024]{1,0:T(8,128)(2,1)S(1)} %copy-done.1, bf16[1024,1536]{1,0:T(8,128)(2,1)S(1)} %copy-done.7), custom_call_target="tpu_custom_call" | custom-call | flops 8000000000 | bytes 6291456 | tf_op jit(solution)/shard_map/attend/pallas_call | solution.py:123
  16.5 0.0 copy-done
  16.5 0.0 copy-done.2
  16.5 0.0 copy-done.4
  16.5 0.0 copy-done.5
  16.5 0.0 copy-done.6
  16.5 34.1 %contrast.1 = (f32[1,4]{1,0:T(1,128)S(1)}, f32[4,1024]{1,0:T(4,128)S(1)}) custom-call(s32[256]{0:T(256)S(1)} %copy-done.5, s32[4]{0:T(128)S(1)} %copy-done.6, s32[1,1024]{1,0:T(1,128)S(1)} %copy-done.3, bf16[1024,1024]{1,0:T(8,128)(2,1)S(1)} %copy-done.1, bf16[1024,512]{1,0:T(8,128)(2,1)S(1)} %attend.1.ctx_ref, bf16[512,1024]{1,0:T(8,128)(2,1)S(1)} %copy-done.2, ...), custom_call_target="tpu_custom_call" | custom-call | tf_op jit(solution)/shard_map/contrast/pallas_call | solution.py:362
  50.6 0.5 copy.12
  51.1 0.6 %copy.13 = f32[4,1024]{1,0:T(4,128)} copy(f32[4,1024]{1,0:T(4,128)S(1)} %get-tuple-element.9) | data formatting | bytes 32768
Async XLA Ops:
  0.6 1.6 %copy-start.1 = (bf16[1024,1024]{1,0:T(8,128)(2,1)S(1)}, bf16[1024,1024]{1,0:T(8,128)(2,1)}, u32[]{:S(2)}) copy-start(bf16[1024,1024]{1,0:T(8,128)(2,1)} %tok_ref.1) | copy-start | bytes 6291460
  2.2 0.7 %copy-start.3 = (s32[1,1024]{1,0:T(1,128)S(1)}, s32[1,1024]{1,0:T(1,128)}, u32[]{:S(2)}) copy-start(s32[1,1024]{1,0:T(1,128)} %seg_ref.3) | copy-start | bytes 12292
  2.9 1.9 %copy-start.7 = (bf16[1024,1536]{1,0:T(8,128)(2,1)S(1)}, bf16[1024,1536]{1,0:T(8,128)(2,1)}, u32[]{:S(2)}) copy-start(bf16[1024,1536]{1,0:T(8,128)(2,1)} %wqkv_hbm.1) | copy-start | bytes 9437188
  4.8 11.7 %copy-start = (bf16[1024,2048]{1,0:T(8,128)(2,1)S(1)}, bf16[1024,2048]{1,0:T(8,128)(2,1)}, u32[]{:S(2)}) copy-start(bf16[1024,2048]{1,0:T(8,128)(2,1)} %w_ref.1) | copy-start | bytes 12582916
  4.8 11.7 %copy-start.2 = (bf16[512,1024]{1,0:T(8,128)(2,1)S(1)}, bf16[512,1024]{1,0:T(8,128)(2,1)}, u32[]{:S(2)}) copy-start(bf16[512,1024]{1,0:T(8,128)(2,1)} %wout_ref.1) | copy-start | bytes 3145732
  4.8 11.7 %copy-start.4 = (f32[1024]{0:T(1024)S(1)}, f32[1024]{0:T(1024)}, u32[]{:S(2)}) copy-start(f32[1024]{0:T(1024)} %param.14) | copy-start | bytes 12292
  4.8 11.7 %copy-start.5 = (s32[256]{0:T(256)S(1)}, s32[256]{0:T(256)}, u32[]{:S(2)}) copy-start(s32[256]{0:T(256)} %counts_ref.1) | copy-start | bytes 3076
  4.8 11.7 %copy-start.6 = (s32[4]{0:T(128)S(1)}, s32[4]{0:T(128)}, u32[]{:S(2)}) copy-start(s32[4]{0:T(128)} %pos_ref.1) | copy-start | bytes 52

commit v3 on v2

--- a/solution.py
+++ b/solution.py
@@ -146,12 +146,13 @@
 
 
 def loss_kernel(
-    n_a, n_b, slots,
+    n_z, n_y, n_x, slots,
     counts_ref, pos_ref, seg_ref, tok_ref, ctx_ref, wout_ref, gain_ref, w_ref, loss_ref, grad_ref,
-    mine_s, colp, rowp, colm, rowm, drow, dcol, yrecv, ysend, mcol, mrow, mdr, mdc,
-    sum_s, p_s, unit_s, emb_s, wt_s, stack,
-    s_colp, r_colp, s_rowp, r_rowp, s_colm, r_colm, s_rowm, r_rowm, s_dr, r_dr, s_dc, r_dc, s_y, r_y,
+    mine_s, colp, rowp, drow, dcol, yrecv, ysend, mdr, mdc,
+    sum_s, p_s, unit_s, emb_s, wt_s,
+    s_colp, r_colp, s_rowp, r_rowp, s_dr, r_dr, s_dc, r_dc, s_y, r_y,
 ):
+    n_a, n_b = n_z * 2, n_y * n_x
     me = lax.axis_index("dp")
     core, b, z = me % 2, (me // 2) % n_b, me // (2 * n_b)
     a = z * 2 + core
@@ -160,79 +161,64 @@
     r_rows = slots * n_b
     c_cols = slots * n_a
 
-    def row_peer(k):
-        o = (b + k) % n_b
-        return o, z * (2 * n_b) + o * 2 + core
-
-    def col_peer(k):
-        o = (a + k) % n_a
-        return o, (o // 2) * (2 * n_b) + b * 2 + o % 2
+    def ring(d, n):
+        return min(d, n - d)
+
+    row_peers = []
+    for dy in range(n_y):
+        for dx in range(n_x):
+            o = (b // n_x + dy) % n_y * n_x + (b % n_x + dx) % n_x
+            row_peers.append((2 * ring(dy, n_y) + 2 * ring(dx, n_x), o, z * (2 * n_b) + o * 2 + core))
+    col_peers = []
+    for dz in range(n_z):
+        for dc in range(2):
+            o = (z + dz) % n_z * 2 + (core + dc) % 2
+            col_peers.append((2 * ring(dz, n_z) + dc, o, (o // 2) * (2 * n_b) + b * 2 + o % 2))
+    row_peers, col_peers = row_peers[1:], col_peers[1:]
 
     barrier = pltpu.get_barrier_semaphore()
-
-    def greet(peer):
-        def step(k, _):
-            pl.semaphore_signal(barrier, inc=1, device_id=(peer(k)[1],), device_id_type=MESH)
-            return 0
-
-        return step
-
-    lax.fori_loop(1, n_b, greet(row_peer), 0)
-    lax.fori_loop(1, n_a, greet(col_peer), 0)
-
-    def exchange(peer, n, mine, source, dest, send, recv):
-        def copy(k):
-            o, device = peer(k)
-            return pltpu.make_async_remote_copy(
-                src_ref=source(o), dst_ref=dest.at[mine], send_sem=send.at[k], recv_sem=recv.at[mine],
-                device_id=(device,), device_id_type=MESH,
-            )
-
-        def start():
-            def step(k, _):
-                copy(k).start()
-                return 0
-
-            lax.fori_loop(1, n, step, 0)
-
-        def arrive():
-            def step(k, _):
-                o, device = peer(k)
-                pltpu.make_async_remote_copy(
-                    src_ref=source(o), dst_ref=dest.at[o], send_sem=send.at[k], recv_sem=recv.at[o],
-                    device_id=(device,), device_id_type=MESH,
-                ).wait_recv()
-                return 0
-
-            lax.fori_loop(1, n, step, 0)
-
-        def drain():
-            def step(k, _):
-                copy(k).wait_send()
-                return 0
-
-            lax.fori_loop(1, n, step, 0)
-
-        return start, arrive, drain
-
-    x_colp = exchange(col_peer, n_a, a, lambda o: mine_s, colp, s_colp, r_colp)
-    x_rowp = exchange(row_peer, n_b, b, lambda o: mine_s, rowp, s_rowp, r_rowp)
-    x_colm = exchange(col_peer, n_a, a, lambda o: mcol, colm, s_colm, r_colm)
-    x_rowm = exchange(row_peer, n_b, b, lambda o: mrow, rowm, s_rowm, r_rowm)
-    x_dr = exchange(row_peer, n_b, b, lambda o: mdr, drow, s_dr, r_dr)
-    x_dc = exchange(col_peer, n_a, a, lambda o: mdc, dcol, s_dc, r_dc)
-    x_y = exchange(row_peer, n_b, b, lambda o: ysend.at[o], yrecv, s_y, r_y)
+    for _, _, device in row_peers + col_peers:
+        pl.semaphore_signal(barrier, inc=1, device_id=(device,), device_id_type=MESH)
+
+    def exchange(peers, mine, source, dest, send, recv):
+        out = []
+        for k, (hops, o, device) in enumerate(peers):
+            out.append((
+                hops,
+                functools.partial(
+                    pltpu.make_async_remote_copy, src_ref=source(o), dst_ref=dest.at[mine], send_sem=send.at[k],
+                    recv_sem=recv.at[mine], device_id=(device,), device_id_type=MESH,
+                ),
+                functools.partial(
+                    pltpu.make_async_remote_copy, src_ref=source(o), dst_ref=dest.at[o], send_sem=send.at[k],
+                    recv_sem=recv.at[o], device_id=(device,), device_id_type=MESH,
+                ),
+            ))
+        return sorted(out, key=lambda c: -c[0])
+
+    def start(*exchanges):
+        for _, copy, _ in sorted(sum(exchanges, []), key=lambda c: -c[0]):
+            copy().start()
+
+    def arrive(exchange):
+        for _, _, copy in reversed(exchange):
+            copy().wait_recv()
+
+    x_col = exchange(col_peers, a, lambda o: mine_s, colp, s_colp, r_colp)
+    x_row = exchange(row_peers, b, lambda o: mine_s, rowp, s_rowp, r_rowp)
+    x_dr = exchange(row_peers, b, lambda o: mdr, drow, s_dr, r_dr)
+    x_dc = exchange(col_peers, a, lambda o: mdc, dcol, s_dc, r_dc)
+    x_y = exchange(row_peers, b, lambda o: ysend.at[o], yrecv, s_y, r_y)
 
     s_id = iota((slots, 1), 0)
     lane = iota((slots, 128), 1)
     live_own = (s_id < counts_ref[me]).astype(F32)
-    pos_own = jnp.zeros((slots, 1), F32)
+    side = jnp.where(lane == 2, live_own, 0.0)
     for s in range(slots):
-        pos_own = jnp.where(s_id == s, pos_ref[s].astype(F32), pos_own)
-    for ref, first in ((mcol, a * slots), (mrow, b * slots)):
-        here = lane == first + iota((slots, 128), 0)
-        ref[0:1, :] = jnp.sum(jnp.where(here, pos_own, 0.0), axis=0, keepdims=True)
-        ref[1:2, :] = jnp.sum(jnp.where(here, live_own, 0.0), axis=0, keepdims=True)
+        own_row = iota((slots, 128), 0) == s
+        side = jnp.where(own_row & (lane == 0), (pos_ref[s] // 32).astype(F32), side)
+        side = jnp.where(own_row & (lane == 1), (pos_ref[s] % 32).astype(F32), side)
+    mine_s[:, width:] = side.astype(BF16)
 
     tile = min(256, rows)
     sum_s[...] = jnp.zeros_like(sum_s)
@@ -250,13 +236,10 @@
     lax.fori_loop(0, rows // tile, finish, 0)
     sizes = jnp.sum((iota((16, rows), 0) == seg_ref[...]).astype(F32), axis=1, keepdims=True)
     pooled = (sum_s[:slots, :] / sizes[:slots]).astype(BF16)
-    mine_s[...] = pooled
+    mine_s[:, :width] = pooled
 
     pl.semaphore_wait(barrier, n_a + n_b - 2)
-    x_colm[0]()
-    x_rowm[0]()
-    x_colp[0]()
-    x_rowp[0]()
+    start(x_col, x_row)
 
     proj = jnp.dot(pooled, w_ref[...], preferred_element_type=F32)
     rnorm = lax.rsqrt(jnp.sum(proj * proj, axis=1, keepdims=True) + 1e-06)
@@ -268,25 +251,21 @@
         return 0
 
     lax.fori_loop(0, embed // 128, turn, 0)
-    colp[a] = pooled
-    rowp[b] = pooled
-    colm[a] = mcol[...]
-    rowm[b] = mrow[...]
+    colp[a] = mine_s[...]
+    rowp[b] = mine_s[...]
     p_s[...] = jnp.zeros_like(p_s)
-    x_colm[1]()
-    x_rowm[1]()
-    x_colp[1]()
+    arrive(x_row)
+    for o in range(n_b):
+        p_s[128 + o * slots : 128 + (o + 1) * slots, :] = rowp[o].astype(F32)
+    arrive(x_col)
     for o in range(n_a):
         p_s[o * slots : (o + 1) * slots, :] = colp[o].astype(F32)
-    x_rowp[1]()
-    for o in range(n_b):
-        p_s[128 + o * slots : 128 + (o + 1) * slots, :] = rowp[o].astype(F32)
-
-    p_b = p_s[...].astype(BF16)
-    proj_all = jnp.dot(p_b, w_ref[...], preferred_element_type=F32)
+
+    proj_all = jnp.dot(p_s[:, :width].astype(BF16), w_ref[...], preferred_element_type=F32)
     rnorm_all = lax.rsqrt(jnp.sum(proj_all * proj_all, axis=1, keepdims=True) + 1e-06)
     emb_s[...] = (proj_all * rnorm_all).astype(BF16)
-    logits = SCALE * lax.dot_general(emb_s[128 : 128 + r_rows, :], emb_s[:128, :], NT, preferred_element_type=F32)
+    emb_j = emb_s[:128, :]
+    logits = SCALE * lax.dot_general(emb_s[128 : 128 + r_rows, :], emb_j, NT, preferred_element_type=F32)
 
     r = iota((r_rows, 128), 0)
     c = iota((r_rows, 128), 1)
@@ -295,12 +274,14 @@
     id_j = ((o_j // 2) * (2 * n_b) + b * 2 + o_j % 2) * slots + c % slots
     eye = r == c
     square = iota((128, 128), 0) == iota((128, 128), 1)
-    rnorm_j = jnp.sum(jnp.where(square, rnorm_all[:128], 0.0), axis=0, keepdims=True)
-    side_j = jnp.sum(colm[...], axis=0)
-    side_i = jnp.sum(rowm[...], axis=0)
-    pos_j, live_j = side_j[0:1], side_j[1:2] > 0.5
-    pos_i = jnp.sum(jnp.where(eye, side_i[0:1], 0.0), axis=1, keepdims=True)
-    live_i = jnp.sum(jnp.where(eye, side_i[1:2], 0.0), axis=1, keepdims=True) > 0.5
+
+    def along(column):
+        return jnp.sum(jnp.where(square, column, 0.0), axis=0, keepdims=True)
+
+    side_j = p_s[:128, width:]
+    side_i = p_s[128 : 128 + r_rows, width:]
+    pos_i, live_i = side_i[:, 0:1] * 32.0 + side_i[:, 1:2], side_i[:, 2:3] > 0.5
+    pos_j, live_j = along(side_j[:, 0:1] * 32.0 + side_j[:, 1:2]), along(side_j[:, 2:3]) > 0.5
     inside = (c < c_cols) & (id_i != id_j)
     expd = jnp.exp(logits)
     exp_i = jnp.where(inside & live_j, expd, 0.0)
@@ -312,24 +293,23 @@
     mdc[...] = jnp.sum(exp_j, axis=0, keepdims=True)
     mdr[0:1, :] = jnp.sum(jnp.where(eye, part_i, 0.0), axis=0, keepdims=True)
     mdr[1:2, :] = jnp.sum(jnp.where(eye, picked, 0.0), axis=0, keepdims=True)
-    x_dc[0]()
-    x_dr[0]()
+    start(x_dr, x_dc)
     drow[b] = mdr[...]
     dcol[a] = mdc[...]
-    x_dr[1]()
-    x_dc[1]()
+    arrive(x_dr)
+    arrive(x_dc)
     sums_i = jnp.sum(drow[...], axis=0)
     den_j = jnp.sum(dcol[...], axis=0)
     den_i = jnp.sum(jnp.where(eye, sums_i[0:1], 0.0), axis=1, keepdims=True)
     w_i = jnp.where(live_i, exp_i / den_i - hit_i.astype(F32), 0.0)
     den_j = jnp.where(den_j > 0.0, den_j, 1.0)
     w_j = jnp.where(live_j & (c < c_cols), exp_j / den_j - hit_j.astype(F32), 0.0)
-    mix_hi, mix_lo = halves((w_i + w_j) * rnorm_j)
-    p_j = p_b[:128]
-    y = jnp.dot(mix_hi, p_j, preferred_element_type=F32) + jnp.dot(mix_lo, p_j, preferred_element_type=F32)
+    mix = jnp.concatenate(halves(w_i + w_j), axis=0)
+    y = jnp.dot(mix, emb_j, preferred_element_type=F32)
+    y = (y[:r_rows] + y[r_rows:]).astype(BF16)
     for o in range(n_b):
         ysend[o] = y[o * slots : (o + 1) * slots]
-    x_y[0]()
+    start(x_y)
     yrecv[b] = ysend[b]
 
     table = jnp.log(sums_i[0:1]) - sums_i[1:2]
@@ -338,71 +318,63 @@
     loss_lane = jnp.sum(jnp.where(lane == iota((slots, 128), 0), mine, 0.0), axis=0, keepdims=True)
     loss_ref[...] = loss_lane[:, :slots]
 
-    x_y[1]()
-    y_own = jnp.sum(yrecv[...], axis=0)
-    y_hi = y_own.astype(BF16).astype(F32)
-    stack[:slots, :] = y_hi
-    stack[slots:, :] = y_own - y_hi
-    d = jnp.dot(stack[...].astype(BF16), w_ref[...], preferred_element_type=F32)
-    d_emb = SCALE * (d[:slots] + d[slots:])
+    arrive(x_y)
+    d_emb = SCALE * jnp.sum(yrecv[...].astype(F32), axis=0)
     own = unit_s[...]
     radial = jnp.sum(d_emb * own, axis=1, keepdims=True)
     d_proj = ((d_emb - radial * own) * rnorm).astype(BF16)
     grad_ref[...] = jnp.dot(d_proj, wt_s[...], preferred_element_type=F32)
-    for x in (x_colm, x_rowm, x_colp, x_rowp, x_dr, x_dc, x_y):
-        x[2]()
-
-
-def contrast(counts, positives, seg, tokens, ctx, w_out, gain, w_proj, n_a, n_b):
+    for x in (x_col, x_row, x_dr, x_dc, x_y):
+        for _, copy, _ in x:
+            copy().wait_send()
+
+
+def contrast(counts, positives, seg, tokens, ctx, w_out, gain, w_proj, n_z, n_y, n_x):
     slots = positives.shape[0]
+    n_a, n_b = n_z * 2, n_y * n_x
     width, embed = w_proj.shape
     vmem = pl.BlockSpec(memory_space=pltpu.VMEM)
     smem = pl.BlockSpec(memory_space=pltpu.SMEM)
-    sems = [pltpu.SemaphoreType.DMA((n,)) for n in (n_a, n_b, n_a, n_b, n_b, n_a, n_b) for _ in range(2)]
+    sems = [pltpu.SemaphoreType.DMA((n,)) for n in (n_a, n_b, n_b, n_a, n_b) for _ in range(2)]
     return pl.pallas_call(
-        functools.partial(loss_kernel, n_a, n_b, slots),
+        functools.partial(loss_kernel, n_z, n_y, n_x, slots),
         name="contrast",
         out_shape=(jax.ShapeDtypeStruct((1, slots), F32), jax.ShapeDtypeStruct((slots, width), F32)),
         in_specs=[smem, smem] + [vmem] * 6,
         out_specs=(vmem, vmem),
         scratch_shapes=[
-            pltpu.VMEM((slots, width), BF16),
-            pltpu.VMEM((n_a, slots, width), BF16),
-            pltpu.VMEM((n_b, slots, width), BF16),
-            pltpu.VMEM((n_a, 2, 128), F32),
-            pltpu.VMEM((n_b, 2, 128), F32),
+            pltpu.VMEM((slots, width + 128), BF16),
+            pltpu.VMEM((n_a, slots, width + 128), BF16),
+            pltpu.VMEM((n_b, slots, width + 128), BF16),
             pltpu.VMEM((n_b, 2, 128), F32),
             pltpu.VMEM((n_a, 1, 128), F32),
-            pltpu.VMEM((n_b, slots, width), F32),
-            pltpu.VMEM((n_b, slots, width), F32),
-            pltpu.VMEM((2, 128), F32),
-            pltpu.VMEM((2, 128), F32),
+            pltpu.VMEM((n_b, slots, embed), BF16),
+            pltpu.VMEM((n_b, slots, embed), BF16),
             pltpu.VMEM((2, 128), F32),
             pltpu.VMEM((1, 128), F32),
             pltpu.VMEM((16, width), F32),
-            pltpu.VMEM((128 + slots * n_b, width), F32),
+            pltpu.VMEM((128 + slots * n_b, width + 128), F32),
             pltpu.VMEM((slots, embed), F32),
             pltpu.VMEM((128 + slots * n_b, embed), BF16),
             pltpu.VMEM((embed, width), BF16),
-            pltpu.VMEM((2 * slots, width), F32),
             *sems,
         ],
         compiler_params=pltpu.CompilerParams(collective_id=0, has_side_effects=True, vmem_limit_bytes=40 * 2**20),
     )(counts, positives, seg, tokens, ctx, w_out, gain, w_proj)
 
 
-def body(n_a, n_b, tokens, seg_ids, counts, positives, w_qkv, w_out, ln_gain, w_proj):
+def body(grid, tokens, seg_ids, counts, positives, w_qkv, w_out, ln_gain, w_proj):
     slots = positives.shape[0]
-    ctx = attend(seg_ids, tokens, w_qkv, slots)
-    loss, grad = contrast(counts, positives, seg_ids, tokens, ctx, w_out, ln_gain[None, :], w_proj, n_a, n_b)
+    in_hbm = functools.partial(pltpu.with_memory_space_constraint, memory_space=pltpu.HBM)
+    ctx = attend(seg_ids, in_hbm(tokens), in_hbm(w_qkv), slots)
+    loss, grad = contrast(counts, positives, seg_ids, tokens, ctx, w_out, ln_gain[None, :], w_proj, *grid)
     return loss.reshape(slots), grad
 
 
 def solution(mesh):
-    n_b = 16
-    n_a = mesh.size // n_b
+    grid = (mesh.size // 32, 4, 4)
     return jax.shard_map(
-        functools.partial(body, n_a, n_b),
+        functools.partial(body, grid),
         mesh=mesh,
         in_specs=(P("dp", None), P("dp", None), P(), P("dp"), P(), P(), P(), P()),
         out_specs=(P("dp"), P("dp", None)),

time: 52 us -> 47.5 us (0.913)
  local copies, waits for them, and re-layouts: 5.3 us -> 1.82 us
  Pallas kernels: 45.7 us -> 44.9 us
    unnamed x18 -> x16, local copies, waits for them, and re-layouts: 5.3 us -> 1.82 us
    pallas_call x1, Pallas kernels: 34.1 us -> 31.3 us  [contrast(): pl.pallas_call(functools.partial(loss_kernel, n_z, n_y, n_x, slots), name...]
    pallas_call x1, Pallas kernels: 11.7 us -> 13.6 us  [attend(): pl.pallas_call(functools.partial(attend_kernel, slots), name='attend', ou...]
where the time goes in v3:
time: 47.5 us; the launch traced here: 47.4 us
  Pallas kernels  44.9 us (95%)
  local copies, waits for them, and re-layouts  1.82 us (4%)
  between operations  0.73 us (2%)
    pallas_call x1, Pallas kernels, contrast(): pl.pallas_call(functools.partial(loss_kernel, n_z, n_y, n_x, slots), name...  31.3 us
    pallas_call x1, Pallas kernels, attend(): pl.pallas_call(functools.partial(attend_kernel, slots), name='attend', ou...  13.6 us
    unnamed x16, local copies, waits for them, and re-layouts  1.82 us

profile of v3, /device:TPU:1, one launch (start us, length us, event | category | flops | bytes accessed | tf_op | source)
XLA Modules:
  0.0 47.4 jit_solution(448195462022207588)
XLA Ops:
  0.6 0.0 copy-start.3
  0.6 0.7 %copy-done.3 = s32[1,1024]{1,0:T(1,128)S(1)} copy-done((s32[1,1024]{1,0:T(1,128)S(1)}, s32[1,1024]{1,0:T(1,128)}, u32[]{:S(2)}) %copy-start.3) | copy-done | bytes 4120
  1.3 0.0 copy-start
  1.3 0.0 copy-start.1
  1.3 0.0 copy-start.2
  1.3 0.0 copy-start.4
  1.3 0.0 copy-start.5
  1.3 0.0 copy-start.6
  1.4 13.6 %attend.1.ctx_ref = bf16[1024,512]{1,0:T(8,128)(2,1)S(1)} custom-call(s32[1,1024]{1,0:T(1,128)S(1)} %copy-done.3, bf16[1024,1024]{1,0:T(8,128)(2,1)} %tok_ref.1, bf16[1024,1536]{1,0:T(8,128)(2,1)} %wqkv_hbm.1), custom_call_target="tpu_custom_call" | custom-call | flops 8000000000 | bytes 6291456 | tf_op jit(solution)/shard_map/attend/pallas_call | solution.py:123
  14.9 0.0 copy-done
  14.9 0.0 copy-done.1
  14.9 0.0 copy-done.2
  15.0 0.0 copy-done.4
  15.0 0.0 copy-done.5
  15.0 0.0 copy-done.6
  15.0 31.3 %contrast.1 = (f32[1,4]{1,0:T(1,128)S(1)}, f32[4,1024]{1,0:T(4,128)S(1)}) custom-call(s32[256]{0:T(256)S(1)} %copy-done.5, s32[4]{0:T(128)S(1)} %copy-done.6, s32[1,1024]{1,0:T(1,128)S(1)} %copy-done.3, bf16[1024,1024]{1,0:T(8,128)(2,1)S(1)} %copy-done.1, bf16[1024,512]{1,0:T(8,128)(2,1)S(1)} %attend.1.ctx_ref, bf16[512,1024]{1,0:T(8,128)(2,1)S(1)} %copy-done.2, ...), custom_call_target="tpu_custom_call" | custom-call | tf_op jit(solution)/shard_map/contrast/pallas_call | solution.py:339
  46.3 0.5 %copy.12 = f32[4]{0:T(128)} copy(f32[4]{0:T(128)S(1)} %bitcast.3) | data formatting | bytes 32
  46.8 0.6 %copy.13 = f32[4,1024]{1,0:T(4,128)} copy(f32[4,1024]{1,0:T(4,128)S(1)} %get-tuple-element.9) | data formatting | bytes 32768
Async XLA Ops:
  0.6 0.7 %copy-start.3 = (s32[1,1024]{1,0:T(1,128)S(1)}, s32[1,1024]{1,0:T(1,128)}, u32[]{:S(2)}) copy-start(s32[1,1024]{1,0:T(1,128)} %seg_ref.3) | copy-start | bytes 12292
  1.3 13.6 %copy-start = (bf16[1024,2048]{1,0:T(8,128)(2,1)S(1)}, bf16[1024,2048]{1,0:T(8,128)(2,1)}, u32[]{:S(2)}) copy-start(bf16[1024,2048]{1,0:T(8,128)(2,1)} %w_ref.1) | copy-start | bytes 12582916
  1.3 13.6 %copy-start.1 = (bf16[1024,1024]{1,0:T(8,128)(2,1)S(1)}, bf16[1024,1024]{1,0:T(8,128)(2,1)}, u32[]{:S(2)}) copy-start(bf16[1024,1024]{1,0:T(8,128)(2,1)} %tok_ref.1) | copy-start | bytes 6291460
  1.3 13.6 %copy-start.2 = (bf16[512,1024]{1,0:T(8,128)(2,1)S(1)}, bf16[512,1024]{1,0:T(8,128)(2,1)}, u32[]{:S(2)}) copy-start(bf16[512,1024]{1,0:T(8,128)(2,1)} %wout_ref.1) | copy-start | bytes 3145732
  1.3 13.6 %copy-start.4 = (f32[1024]{0:T(1024)S(1)}, f32[1024]{0:T(1024)}, u32[]{:S(2)}) copy-start(f32[1024]{0:T(1024)} %param.14) | copy-start | bytes 12292
  1.3 13.6 %copy-start.5 = (s32[256]{0:T(256)S(1)}, s32[256]{0:T(256)}, u32[]{:S(2)}) copy-start(s32[256]{0:T(256)} %counts_ref.1) | copy-start | bytes 3076
  1.3 13.6 %copy-start.6 = (s32[4]{0:T(128)S(1)}, s32[4]{0:T(128)}, u32[]{:S(2)}) copy-start(s32[4]{0:T(128)} %pos_ref.1) | copy-start | bytes 52

commit v4 on v3

--- a/solution.py
+++ b/solution.py
@@ -21,7 +21,9 @@
     return lax.broadcasted_iota(I32, shape, dim)
 
 
-def attend_kernel(slots, seg_ref, tok_hbm, wqkv_hbm, ctx_ref, tok_ref, wqkv_ref, q_s, kt_s, v_s, qm_s, sem):
+def attend_kernel(
+    slots, seg_hbm, tok_hbm, wqkv_hbm, wout_hbm, wproj_hbm, ctx_ref, tok_ref, wout_ref, wproj_ref, seg_ref, wqkv_ref, q_s, kt_s, v_s, qm_s, sem,
+):
     rows = tok_ref.shape[0]
     inner = ctx_ref.shape[1]
     head_dim = inner // HEADS
@@ -29,6 +31,8 @@
     tile = min(256, rows)
     qtile = 128
 
+    seg_copy = pltpu.make_async_copy(seg_hbm, seg_ref, sem.at[1 + rows // tile])
+    seg_copy.start()
     w_copy = pltpu.make_async_copy(wqkv_hbm, wqkv_ref, sem.at[0])
     w_copy.start()
 
@@ -38,6 +42,7 @@
 
     for t in range(rows // tile):
         tok_copy(t).start()
+    seg_copy.wait()
     seg = seg_ref[...]
 
     sub = iota((128, rows), 0)
@@ -73,49 +78,68 @@
 
     lax.fori_loop(0, rows // tile, project, 0)
 
-    def window(at, first, span):
-        keys = pl.ds(first, span)
+    later = [
+        pltpu.make_async_copy(wout_hbm, wout_ref, sem.at[2 + rows // tile]),
+        pltpu.make_async_copy(wproj_hbm, wproj_ref, sem.at[3 + rows // tile]),
+    ]
+    for copy in later:
+        copy.start()
+
+    def window(tiles, span):
         low = iota((qtile, 128), 1) < head_dim
-        qm = qm_s[at, :]
         scores = []
-        for n in range(HEADS):
-            q = q_s[at, n // 2 * 128 : (n // 2 + 1) * 128]
-            q = jnp.where(low, q, qm) if n % 2 == 0 else jnp.where(low, qm, q)
-            scores.append(jnp.dot(q, kt_s[n, :, keys], preferred_element_type=F32))
+        for at, first in tiles:
+            qm = qm_s[at, :]
+            for n in range(HEADS):
+                q = q_s[at, n // 2 * 128 : (n // 2 + 1) * 128]
+                q = jnp.where(low, q, qm) if n % 2 == 0 else jnp.where(low, qm, q)
+                scores.append(jnp.dot(q, kt_s[n, :, pl.ds(first, span)], preferred_element_type=F32))
         exps = [jnp.exp(s - jnp.max(s, axis=1, keepdims=True)).astype(BF16) for s in scores]
-        outs = [jnp.dot(e, v_s[n, keys, :], preferred_element_type=F32) for n, e in enumerate(exps)]
-        for p in range(pairs):
-            top = jnp.where(low, outs[2 * p], outs[2 * p + 1])
-            den = pltpu.roll(jnp.where(low, outs[2 * p + 1], outs[2 * p]), head_dim, 1)
-            ctx_ref[at, p * 128 : (p + 1) * 128] = (top / den).astype(BF16)
+        outs = []
+        for i, (at, first) in enumerate(tiles):
+            for n in range(HEADS):
+                outs.append(jnp.dot(exps[i * HEADS + n], v_s[n, pl.ds(first, span), :], preferred_element_type=F32))
+        for i, (at, first) in enumerate(tiles):
+            for p in range(pairs):
+                even, odd = outs[i * HEADS + 2 * p], outs[i * HEADS + 2 * p + 1]
+                top = jnp.where(low, even, odd)
+                den = pltpu.roll(jnp.where(low, odd, even), head_dim, 1)
+                ctx_ref[at, p * 128 : (p + 1) * 128] = (top / den).astype(BF16)
+
+    group = min(2, rows // qtile)
 
     def queries(t, _):
-        q0 = t * qtile
-        at = pl.ds(pl.multiple_of(q0, qtile), qtile)
-        lo = jnp.int32(0)
-        hi = jnp.int32(rows)
-        for s in range(1, slots):
-            lo = jnp.where(starts[s] <= q0, starts[s], lo)
-        for s in range(slots - 1, 0, -1):
-            hi = jnp.where(starts[s] >= q0 + qtile, starts[s], hi)
-        lo = lo // 128 * 128
-        spans = [w for w in (512, 768) if w < rows] + [rows]
-        below = jnp.int32(0)
-        for w in spans:
-            fits = hi - lo <= w
-
-            @pl.when(fits & (below == 0))
+        los, width_needed = [], jnp.int32(0)
+        for i in range(group):
+            q0 = (t * group + i) * qtile
+            lo = jnp.int32(0)
+            hi = jnp.int32(rows)
+            for s in range(1, slots):
+                lo = jnp.where(starts[s] <= q0, starts[s], lo)
+            for s in range(slots - 1, 0, -1):
+                hi = jnp.where(starts[s] >= q0 + qtile, starts[s], hi)
+            lo = lo // 128 * 128
+            los.append(lo)
+            width_needed = jnp.maximum(width_needed, hi - lo)
+        spans = [w for w in (384, 512, 640, 768) if w < rows] + [rows]
+        for below, w in zip([0] + spans, spans):
+
+            @pl.when((width_needed > below) & (width_needed <= w))
             def _(w=w):
-                first = 0 if w == rows else pl.multiple_of(jnp.minimum(lo, rows - w), 128)
-                window(at, first, w)
-
-            below = jnp.where(fits, 1, below)
+                tiles = []
+                for i in range(group):
+                    at = pl.ds(pl.multiple_of((t * group + i) * qtile, qtile), qtile)
+                    tiles.append((at, 0 if w == rows else pl.multiple_of(jnp.minimum(los[i], rows - w), 128)))
+                window(tiles, w)
+
         return 0
 
-    lax.fori_loop(0, rows // qtile, queries, 0)
-
-
-def attend(seg, tokens, w_qkv, slots):
+    lax.fori_loop(0, rows // (qtile * group), queries, 0)
+    for copy in later:
+        copy.wait()
+
+
+def attend(seg, tokens, w_qkv, w_out, w_proj, slots):
     rows, width = tokens.shape
     inner = w_qkv.shape[1] // 3
     vmem = pl.BlockSpec(memory_space=pltpu.VMEM)
@@ -123,21 +147,21 @@
     return pl.pallas_call(
         functools.partial(attend_kernel, slots),
         name="attend",
-        out_shape=jax.ShapeDtypeStruct((rows, inner), BF16),
-        in_specs=[vmem, hbm, hbm],
-        out_specs=vmem,
+        out_shape=[jax.ShapeDtypeStruct(x, BF16) for x in ((rows, inner), tokens.shape, w_out.shape, w_proj.shape)],
+        in_specs=[hbm] * 5,
+        out_specs=[vmem] * 4,
         scratch_shapes=[
-            pltpu.VMEM((rows, width), BF16),
+            pltpu.VMEM((1, rows), I32),
             pltpu.VMEM((width, 3 * inner), BF16),
             pltpu.VMEM((rows, inner), BF16),
             pltpu.VMEM((HEADS, 128, rows), BF16),
             pltpu.VMEM((HEADS, rows, 128), BF16),
             pltpu.VMEM((rows, 128), BF16),
-            pltpu.SemaphoreType.DMA((1 + rows // min(256, rows),)),
+            pltpu.SemaphoreType.DMA((4 + rows // min(256, rows),)),
         ],
         compiler_params=pltpu.CompilerParams(vmem_limit_bytes=40 * 2**20),
         cost_estimate=pl.CostEstimate(flops=8 * 10**9, bytes_accessed=6 * 2**20, transcendentals=4 * 10**6),
-    )(seg, tokens, w_qkv)
+    )(seg, tokens, w_qkv, w_out, w_proj)
 
 
 def halves(x):
@@ -149,7 +173,7 @@
     n_z, n_y, n_x, slots,
     counts_ref, pos_ref, seg_ref, tok_ref, ctx_ref, wout_ref, gain_ref, w_ref, loss_ref, grad_ref,
     mine_s, colp, rowp, drow, dcol, yrecv, ysend, mdr, mdc,
-    sum_s, p_s, unit_s, emb_s, wt_s,
+    p_s, unit_s, emb_s, wt_s,
     s_colp, r_colp, s_rowp, r_rowp, s_dr, r_dr, s_dc, r_dc, s_y, r_y,
 ):
     n_a, n_b = n_z * 2, n_y * n_x
@@ -212,30 +236,38 @@
 
     s_id = iota((slots, 1), 0)
     lane = iota((slots, 128), 1)
-    live_own = (s_id < counts_ref[me]).astype(F32)
-    side = jnp.where(lane == 2, live_own, 0.0)
-    for s in range(slots):
-        own_row = iota((slots, 128), 0) == s
-        side = jnp.where(own_row & (lane == 0), (pos_ref[s] // 32).astype(F32), side)
-        side = jnp.where(own_row & (lane == 1), (pos_ref[s] % 32).astype(F32), side)
+    n_devices = counts_ref.shape[1]
+    my_count = jnp.sum(jnp.where(iota((1, n_devices), 1) == me, counts_ref[...], 0).astype(F32), axis=1, keepdims=True)
+    live_own = (s_id.astype(F32) < my_count).astype(F32)
+    diagonal = iota((slots, slots), 0) == iota((slots, slots), 1)
+
+    def down(values):
+        return jnp.sum(jnp.where(diagonal, values.astype(F32), 0.0), axis=1, keepdims=True)
+
+    places = pos_ref[...]
+    side = jnp.where(lane == 0, down(places >> 5), jnp.where(lane == 1, down(places & 31), 0.0))
+    side = jnp.where(lane == 2, live_own, side)
     mine_s[:, width:] = side.astype(BF16)
 
     tile = min(256, rows)
-    sum_s[...] = jnp.zeros_like(sum_s)
-
-    def finish(t, _):
-        at = pl.ds(pl.multiple_of(t * tile, tile), tile)
-        resid = tok_ref[at, :].astype(F32) + jnp.dot(ctx_ref[at, :], wout_ref[...], preferred_element_type=F32)
+
+    def mix_in(t):
+        at = pl.ds(t * tile, tile)
+        return tok_ref[at, :].astype(F32) + jnp.dot(ctx_ref[at, :], wout_ref[...], preferred_element_type=F32)
+
+    def norm(resid):
         centre = resid - jnp.sum(resid, axis=1, keepdims=True) * (1.0 / width)
         variance = jnp.sum(centre * centre, axis=1, keepdims=True) * (1.0 / width)
-        hidden = (centre * lax.rsqrt(variance + 1e-05) * gain_ref[...]).astype(BF16)
-        member = (iota((16, tile), 0) == seg_ref[:, at]).astype(F32).astype(BF16)
-        sum_s[...] += jnp.dot(member, hidden, preferred_element_type=F32)
-        return 0
-
-    lax.fori_loop(0, rows // tile, finish, 0)
+        return (centre * lax.rsqrt(variance + 1e-05) * gain_ref[...]).astype(BF16)
+
+    def pool(t, hidden):
+        member = (iota((16, tile), 0) == seg_ref[:, pl.ds(t * tile, tile)]).astype(F32).astype(BF16)
+        return jnp.dot(member, hidden, preferred_element_type=F32)
+
+    resids = [mix_in(t) for t in range(rows // tile)]
+    sums = sum(pool(t, norm(resid)) for t, resid in enumerate(resids))
     sizes = jnp.sum((iota((16, rows), 0) == seg_ref[...]).astype(F32), axis=1, keepdims=True)
-    pooled = (sum_s[:slots, :] / sizes[:slots]).astype(BF16)
+    pooled = (sums[:slots] / sizes[:slots]).astype(BF16)
     mine_s[:, :width] = pooled
 
     pl.semaphore_wait(barrier, n_a + n_b - 2)
@@ -330,17 +362,16 @@
 
 
 def contrast(counts, positives, seg, tokens, ctx, w_out, gain, w_proj, n_z, n_y, n_x):
-    slots = positives.shape[0]
+    slots = positives.shape[1]
     n_a, n_b = n_z * 2, n_y * n_x
     width, embed = w_proj.shape
     vmem = pl.BlockSpec(memory_space=pltpu.VMEM)
-    smem = pl.BlockSpec(memory_space=pltpu.SMEM)
     sems = [pltpu.SemaphoreType.DMA((n,)) for n in (n_a, n_b, n_b, n_a, n_b) for _ in range(2)]
     return pl.pallas_call(
         functools.partial(loss_kernel, n_z, n_y, n_x, slots),
         name="contrast",
         out_shape=(jax.ShapeDtypeStruct((1, slots), F32), jax.ShapeDtypeStruct((slots, width), F32)),
-        in_specs=[smem, smem] + [vmem] * 6,
+        in_specs=[vmem] * 8,
         out_specs=(vmem, vmem),
         scratch_shapes=[
             pltpu.VMEM((slots, width + 128), BF16),
@@ -352,7 +383,6 @@
             pltpu.VMEM((n_b, slots, embed), BF16),
             pltpu.VMEM((2, 128), F32),
             pltpu.VMEM((1, 128), F32),
-            pltpu.VMEM((16, width), F32),
             pltpu.VMEM((128 + slots * n_b, width + 128), F32),
             pltpu.VMEM((slots, embed), F32),
             pltpu.VMEM((128 + slots * n_b, embed), BF16),
@@ -366,8 +396,8 @@
 def body(grid, tokens, seg_ids, counts, positives, w_qkv, w_out, ln_gain, w_proj):
     slots = positives.shape[0]
     in_hbm = functools.partial(pltpu.with_memory_space_constraint, memory_space=pltpu.HBM)
-    ctx = attend(seg_ids, in_hbm(tokens), in_hbm(w_qkv), slots)
-    loss, grad = contrast(counts, positives, seg_ids, tokens, ctx, w_out, ln_gain[None, :], w_proj, *grid)
+    ctx, tokens, w_out, w_proj = attend(*map(in_hbm, (seg_ids, tokens, w_qkv, w_out, w_proj)), slots)
+    loss, grad = contrast(counts[None, :], positives[None, :], seg_ids, tokens, ctx, w_out, ln_gain[None, :], w_proj, *grid)
     return loss.reshape(slots), grad
 
 

time: 47.5 us -> 46.1 us (0.971)
  Pallas kernels: 44.9 us -> 44 us
  local copies, waits for them, and re-layouts: 1.82 us -> 1.13 us
    pallas_call x1, Pallas kernels: 13.6 us -> 11.8 us  [attend(): pl.pallas_call(functools.partial(attend_kernel, slots), name='attend', ou...]
    pallas_call x1, Pallas kernels: 31.3 us -> 32.3 us  [contrast(): pl.pallas_call(functools.partial(loss_kernel, n_z, n_y, n_x, slots), name...]
    unnamed x16 -> x10, local copies, waits for them, and re-layouts: 1.82 us -> 1.13 us
where the time goes in v4:
time: 46.1 us; the launch traced here: 45.9 us
  Pallas kernels  44 us (95%)
  local copies, waits for them, and re-layouts  1.13 us (2%)
  between operations  0.71 us (2%)
    pallas_call x1, Pallas kernels, contrast(): pl.pallas_call(functools.partial(loss_kernel, n_z, n_y, n_x, slots), name...  32.3 us
    pallas_call x1, Pallas kernels, attend(): pl.pallas_call(functools.partial(attend_kernel, slots), name='attend', ou...  11.8 us
    unnamed x10, local copies, waits for them, and re-layouts  1.13 us

profile of v4, /device:TPU:1, one launch (start us, length us, event | category | flops | bytes accessed | tf_op | source)
XLA Modules:
  0.0 45.9 jit_solution(4939482316710973996)
XLA Ops:
  0.6 0.0 copy-start
  0.6 0.0 copy-start.1
  0.7 0.0 copy-start.2
  0.7 0.0 copy-start.3
  0.7 11.8 %attend.1 = (bf16[1024,512]{1,0:T(8,128)(2,1)S(1)}, bf16[1024,1024]{1,0:T(8,128)(2,1)S(1)}, bf16[512,1024]{1,0:T(8,128)(2,1)S(1)}, bf16[1024,2048]{1,0:T(8,128)(2,1)S(1)}) custom-call(s32[1,1024]{1,0:T(1,128)} %seg_ref.1, bf16[1024,1024]{1,0:T(8,128)(2,1)} %tok_hbm.1, bf16[1024,1536]{1,0:T(8,128)(2,1)} %wqkv_hbm.1, bf16[512,1024]{1,0:T(8,128)(2,1)} %wout_hbm.1, ...), custom_call_target="tpu_custom_call" | custom-call | flops 8000000000 | bytes 6291456 | tf_op jit(solution)/shard_map/attend/pallas_call | solution.py:147
  12.5 0.0 copy-done
  12.5 0.0 copy-done.1
  12.5 0.0 copy-done.2
  12.5 0.0 copy-done.3
  12.5 32.3 %contrast.1 = (f32[1,4]{1,0:T(1,128)S(1)}, f32[4,1024]{1,0:T(4,128)S(1)}) custom-call(s32[1,256]{1,0:T(1,128)S(1)} %bitcast.5, s32[1,4]{1,0:T(1,128)S(1)} %bitcast.6, s32[1,1024]{1,0:T(1,128)S(1)} %copy-done, bf16[1024,1024]{1,0:T(8,128)(2,1)S(1)} %get-tuple-element.8.tok_ref, bf16[1024,512]{1,0:T(8,128)(2,1)S(1)} %get-tuple-element.9.ctx_ref, ...), custom_call_target="tpu_custom_call" | custom-call | tf_op jit(solution)/shard_map/contrast/pallas_call | solution.py:370
  44.8 0.5 %copy.12 = f32[4]{0:T(128)} copy(f32[4]{0:T(128)S(1)} %bitcast.7) | data formatting | bytes 32
  45.3 0.6 %copy.13 = f32[4,1024]{1,0:T(4,128)} copy(f32[4,1024]{1,0:T(4,128)S(1)} %get-tuple-element.17) | data formatting | bytes 32768
Async XLA Ops:
  0.6 11.8 %copy-start = (s32[1,1024]{1,0:T(1,128)S(1)}, s32[1,1024]{1,0:T(1,128)}, u32[]{:S(2)}) copy-start(s32[1,1024]{1,0:T(1,128)} %seg_ref.1) | copy-start | bytes 12292
  0.6 11.8 %copy-start.1 = (f32[1024]{0:T(1024)S(1)}, f32[1024]{0:T(1024)}, u32[]{:S(2)}) copy-start(f32[1024]{0:T(1024)} %param.14) | copy-start | bytes 12292
  0.7 11.8 %copy-start.2 = (s32[256]{0:T(256)S(1)}, s32[256]{0:T(256)}, u32[]{:S(2)}) copy-start(s32[256]{0:T(256)} %param.10) | copy-start | bytes 3076
  0.7 11.8 %copy-start.3 = (s32[4]{0:T(128)S(1)}, s32[4]{0:T(128)}, u32[]{:S(2)}) copy-start(s32[4]{0:T(128)} %param.11) | copy-start | bytes 52

commit v5 on v4

--- a/solution.py
+++ b/solution.py
@@ -106,7 +106,7 @@
                 den = pltpu.roll(jnp.where(low, odd, even), head_dim, 1)
                 ctx_ref[at, p * 128 : (p + 1) * 128] = (top / den).astype(BF16)
 
-    group = min(2, rows // qtile)
+    group = 1
 
     def queries(t, _):
         los, width_needed = [], jnp.int32(0)
@@ -121,7 +121,7 @@
             lo = lo // 128 * 128
             los.append(lo)
             width_needed = jnp.maximum(width_needed, hi - lo)
-        spans = [w for w in (384, 512, 640, 768) if w < rows] + [rows]
+        spans = [w for w in (256, 384, 512, 640, 768, 896) if w < rows] + [rows]
         for below, w in zip([0] + spans, spans):
 
             @pl.when((width_needed > below) & (width_needed <= w))
@@ -393,11 +393,34 @@
     )(counts, positives, seg, tokens, ctx, w_out, gain, w_proj)
 
 
+def deliver_kernel(loss_ref, grad_ref, loss_hbm, grad_hbm, sem):
+    copies = [pltpu.make_async_copy(loss_ref, loss_hbm, sem.at[0]), pltpu.make_async_copy(grad_ref, grad_hbm, sem.at[1])]
+    for copy in copies:
+        copy.start()
+    for copy in copies:
+        copy.wait()
+
+
+def deliver(loss, grad):
+    vmem = pl.BlockSpec(memory_space=pltpu.VMEM)
+    hbm = pl.BlockSpec(memory_space=pltpu.HBM)
+    return pl.pallas_call(
+        deliver_kernel,
+        name="deliver",
+        out_shape=(jax.ShapeDtypeStruct(loss.shape, F32), jax.ShapeDtypeStruct(grad.shape, F32)),
+        in_specs=[vmem, vmem],
+        out_specs=(hbm, hbm),
+        scratch_shapes=[pltpu.SemaphoreType.DMA((2,))],
+        compiler_params=pltpu.CompilerParams(vmem_limit_bytes=2**20),
+    )(loss, grad)
+
+
 def body(grid, tokens, seg_ids, counts, positives, w_qkv, w_out, ln_gain, w_proj):
     slots = positives.shape[0]
     in_hbm = functools.partial(pltpu.with_memory_space_constraint, memory_space=pltpu.HBM)
     ctx, tokens, w_out, w_proj = attend(*map(in_hbm, (seg_ids, tokens, w_qkv, w_out, w_proj)), slots)
     loss, grad = contrast(counts[None, :], positives[None, :], seg_ids, tokens, ctx, w_out, ln_gain[None, :], w_proj, *grid)
+    loss, grad = deliver(loss, grad)
     return loss.reshape(slots), grad
 
 

time: 46.1 us -> 45.2 us (0.980)
  local copies, waits for them, and re-layouts: 1.13 us -> 0.02 us
    unnamed x10 -> x8, local copies, waits for them, and re-layouts: 1.13 us -> 0.02 us
    pallas_call x0 -> x1, Pallas kernels: none -> 0.63 us  [deliver(): pl.pallas_call(deliver_kernel, name='deliver', out_shape=(jax.ShapeDtypeS...]
where the time goes in v5:
time: 45.2 us; the launch traced here: 45.3 us
  Pallas kernels  44.4 us (98%)
  between operations  0.87 us (2%)
    pallas_call x1, Pallas kernels, contrast(): pl.pallas_call(functools.partial(loss_kernel, n_z, n_y, n_x, slots), name...  32.4 us
    pallas_call x1, Pallas kernels, attend(): pl.pallas_call(functools.partial(attend_kernel, slots), name='attend', ou...  11.4 us

profile of v5, /device:TPU:1, one launch (start us, length us, event | category | flops | bytes accessed | tf_op | source)
XLA Modules:
  0.0 45.3 jit_solution(18323968099503051426)
XLA Ops:
  0.6 0.0 copy-start
  0.6 0.0 copy-start.1
  0.7 0.0 copy-start.2
  0.7 0.0 copy-start.3
  0.7 11.4 %attend.1 = (bf16[1024,512]{1,0:T(8,128)(2,1)S(1)}, bf16[1024,1024]{1,0:T(8,128)(2,1)S(1)}, bf16[512,1024]{1,0:T(8,128)(2,1)S(1)}, bf16[1024,2048]{1,0:T(8,128)(2,1)S(1)}) custom-call(s32[1,1024]{1,0:T(1,128)} %seg_ref.1, bf16[1024,1024]{1,0:T(8,128)(2,1)} %tok_hbm.1, bf16[1024,1536]{1,0:T(8,128)(2,1)} %wqkv_hbm.1, bf16[512,1024]{1,0:T(8,128)(2,1)} %wout_hbm.1, ...), custom_call_target="tpu_custom_call" | custom-call | flops 8000000000 | bytes 6291456 | tf_op jit(solution)/shard_map/attend/pallas_call | solution.py:147
  12.1 0.0 copy-done
  12.1 0.0 copy-done.1
  12.1 0.0 copy-done.2
  12.1 0.0 copy-done.3
  12.1 32.4 %contrast.1 = (f32[1,4]{1,0:T(1,128)S(1)}, f32[4,1024]{1,0:T(4,128)S(1)}) custom-call(s32[1,256]{1,0:T(1,128)S(1)} %bitcast.5, s32[1,4]{1,0:T(1,128)S(1)} %bitcast.6, s32[1,1024]{1,0:T(1,128)S(1)} %copy-done, bf16[1024,1024]{1,0:T(8,128)(2,1)S(1)} %get-tuple-element.10.tok_ref, bf16[1024,512]{1,0:T(8,128)(2,1)S(1)} %get-tuple-element.11.ctx_ref, ...), custom_call_target="tpu_custom_call" | custom-call | tf_op jit(solution)/shard_map/contrast/pallas_call | solution.py:370
  44.5 0.6 %deliver.1 = (f32[1,4]{1,0:T(1,128)}, f32[4,1024]{1,0:T(4,128)}) custom-call(f32[1,4]{1,0:T(1,128)S(1)} %get-tuple-element.14.loss_ref, f32[4,1024]{1,0:T(4,128)S(1)} %get-tuple-element.15.grad_ref), custom_call_target="tpu_custom_call" | custom-call | tf_op jit(solution)/shard_map/deliver/pallas_call | solution.py:407
Async XLA Ops:
  0.6 11.4 %copy-start = (s32[1,1024]{1,0:T(1,128)S(1)}, s32[1,1024]{1,0:T(1,128)}, u32[]{:S(2)}) copy-start(s32[1,1024]{1,0:T(1,128)} %seg_ref.1) | copy-start | bytes 12292
  0.6 11.4 %copy-start.1 = (f32[1024]{0:T(1024)S(1)}, f32[1024]{0:T(1024)}, u32[]{:S(2)}) copy-start(f32[1024]{0:T(1024)} %param.14) | copy-start | bytes 12292
  0.7 11.4 %copy-start.2 = (s32[256]{0:T(256)S(1)}, s32[256]{0:T(256)}, u32[]{:S(2)}) copy-start(s32[256]{0:T(256)} %param.10) | copy-start | bytes 3076
  0.7 11.4 %copy-start.3 = (s32[4]{0:T(128)S(1)}, s32[4]{0:T(128)}, u32[]{:S(2)}) copy-start(s32[4]{0:T(128)} %param.11) | copy-start | bytes 52

commit v6 on v5

--- a/solution.py
+++ b/solution.py
@@ -9,6 +9,7 @@
 
 HEADS = 8
 SCALE = 20.0
+TILE = 128
 FAR = -1e30
 MESH = pl.DeviceIdType.MESH
 F32 = jnp.float32
@@ -21,15 +22,34 @@
     return lax.broadcasted_iota(I32, shape, dim)
 
 
+def context(queries, far, kt_ref, v_ref, keys):
+    pairs = HEADS // 2
+    low = iota((TILE, 128), 1) < 64
+    scores = []
+    for n in range(HEADS):
+        q = queries[:, n // 2 * 128 : (n // 2 + 1) * 128]
+        q = jnp.where(low, q, far) if n % 2 == 0 else jnp.where(low, far, q)
+        scores.append(jnp.dot(q, kt_ref[n, :, keys], preferred_element_type=F32))
+    exps = [jnp.exp(s - jnp.max(s, axis=1, keepdims=True)).astype(BF16) for s in scores]
+    outs = [jnp.dot(e, v_ref[n, keys, :], preferred_element_type=F32) for n, e in enumerate(exps)]
+    done = []
+    for p in range(pairs):
+        even, odd = outs[2 * p], outs[2 * p + 1]
+        top = jnp.where(low, even, odd)
+        den = pltpu.roll(jnp.where(low, odd, even), 64, 1)
+        done.append((top / den).astype(BF16))
+    return jnp.concatenate(done, axis=1)
+
+
 def attend_kernel(
-    slots, seg_hbm, tok_hbm, wqkv_hbm, wout_hbm, wproj_hbm, ctx_ref, tok_ref, wout_ref, wproj_ref, seg_ref, wqkv_ref, q_s, kt_s, v_s, qm_s, sem,
+    slots, seg_hbm, tok_hbm, wqkv_hbm, wout_hbm, wproj_hbm, ctx_ref, tok_ref, wout_ref, wproj_ref, kt_s, v_s,
+    ql_ref, qml_ref, seg_ref, wqkv_ref, q_s, qm_s, sem,
 ):
     rows = tok_ref.shape[0]
     inner = ctx_ref.shape[1]
     head_dim = inner // HEADS
     pairs = HEADS // 2
     tile = min(256, rows)
-    qtile = 128
 
     seg_copy = pltpu.make_async_copy(seg_hbm, seg_ref, sem.at[1 + rows // tile])
     seg_copy.start()
@@ -85,56 +105,32 @@
     for copy in later:
         copy.start()
 
-    def window(tiles, span):
-        low = iota((qtile, 128), 1) < head_dim
-        scores = []
-        for at, first in tiles:
-            qm = qm_s[at, :]
-            for n in range(HEADS):
-                q = q_s[at, n // 2 * 128 : (n // 2 + 1) * 128]
-                q = jnp.where(low, q, qm) if n % 2 == 0 else jnp.where(low, qm, q)
-                scores.append(jnp.dot(q, kt_s[n, :, pl.ds(first, span)], preferred_element_type=F32))
-        exps = [jnp.exp(s - jnp.max(s, axis=1, keepdims=True)).astype(BF16) for s in scores]
-        outs = []
-        for i, (at, first) in enumerate(tiles):
-            for n in range(HEADS):
-                outs.append(jnp.dot(exps[i * HEADS + n], v_s[n, pl.ds(first, span), :], preferred_element_type=F32))
-        for i, (at, first) in enumerate(tiles):
-            for p in range(pairs):
-                even, odd = outs[i * HEADS + 2 * p], outs[i * HEADS + 2 * p + 1]
-                top = jnp.where(low, even, odd)
-                den = pltpu.roll(jnp.where(low, odd, even), head_dim, 1)
-                ctx_ref[at, p * 128 : (p + 1) * 128] = (top / den).astype(BF16)
-
-    group = 1
-
     def queries(t, _):
-        los, width_needed = [], jnp.int32(0)
-        for i in range(group):
-            q0 = (t * group + i) * qtile
-            lo = jnp.int32(0)
-            hi = jnp.int32(rows)
-            for s in range(1, slots):
-                lo = jnp.where(starts[s] <= q0, starts[s], lo)
-            for s in range(slots - 1, 0, -1):
-                hi = jnp.where(starts[s] >= q0 + qtile, starts[s], hi)
-            lo = lo // 128 * 128
-            los.append(lo)
-            width_needed = jnp.maximum(width_needed, hi - lo)
+        q0 = t * TILE
+        at = pl.ds(pl.multiple_of(q0, TILE), TILE)
+        lo = jnp.int32(0)
+        hi = jnp.int32(rows)
+        for s in range(1, slots):
+            lo = jnp.where(starts[s] <= q0, starts[s], lo)
+        for s in range(slots - 1, 0, -1):
+            hi = jnp.where(starts[s] >= q0 + TILE, starts[s], hi)
+        lo = lo // 128 * 128
+        needed = hi - lo
         spans = [w for w in (256, 384, 512, 640, 768, 896) if w < rows] + [rows]
         for below, w in zip([0] + spans, spans):
 
-            @pl.when((width_needed > below) & (width_needed <= w))
+            @pl.when((needed > below) & (needed <= w))
             def _(w=w):
-                tiles = []
-                for i in range(group):
-                    at = pl.ds(pl.multiple_of((t * group + i) * qtile, qtile), qtile)
-                    tiles.append((at, 0 if w == rows else pl.multiple_of(jnp.minimum(los[i], rows - w), 128)))
-                window(tiles, w)
+                first = 0 if w == rows else pl.multiple_of(jnp.minimum(lo, rows - w), 128)
+                keys = pl.ds(first, w)
+                ctx_ref[at, :] = context(q_s[at, :], qm_s[at, :], kt_s, v_s, keys)
 
         return 0
 
-    lax.fori_loop(0, rows // (qtile * group), queries, 0)
+    lax.fori_loop(0, rows // TILE - 1, queries, 0)
+    last = pl.ds(rows - TILE, TILE)
+    ql_ref[...] = q_s[last, :]
+    qml_ref[...] = qm_s[last, :]
     for copy in later:
         copy.wait()
 
@@ -147,15 +143,19 @@
     return pl.pallas_call(
         functools.partial(attend_kernel, slots),
         name="attend",
-        out_shape=[jax.ShapeDtypeStruct(x, BF16) for x in ((rows, inner), tokens.shape, w_out.shape, w_proj.shape)],
+        out_shape=[
+            jax.ShapeDtypeStruct(x, BF16)
+            for x in (
+                (rows, inner), tokens.shape, w_out.shape, w_proj.shape,
+                (HEADS, 128, rows), (HEADS, rows, 128), (TILE, inner), (TILE, 128),
+            )
+        ],
         in_specs=[hbm] * 5,
-        out_specs=[vmem] * 4,
+        out_specs=[vmem] * 8,
         scratch_shapes=[
             pltpu.VMEM((1, rows), I32),
             pltpu.VMEM((width, 3 * inner), BF16),
             pltpu.VMEM((rows, inner), BF16),
-            pltpu.VMEM((HEADS, 128, rows), BF16),
-            pltpu.VMEM((HEADS, rows, 128), BF16),
             pltpu.VMEM((rows, 128), BF16),
             pltpu.SemaphoreType.DMA((4 + rows // min(256, rows),)),
         ],
@@ -171,7 +171,8 @@
 
 def loss_kernel(
     n_z, n_y, n_x, slots,
-    counts_ref, pos_ref, seg_ref, tok_ref, ctx_ref, wout_ref, gain_ref, w_ref, loss_ref, grad_ref,
+    counts_ref, pos_ref, seg_ref, tok_ref, ctx_ref, wout_ref, gain_ref, w_ref,
+    kt_ref, v_ref, ql_ref, qml_ref, loss_ref, grad_ref,
     mine_s, colp, rowp, drow, dcol, yrecv, ysend, mdr, mdc,
     p_s, unit_s, emb_s, wt_s,
     s_colp, r_colp, s_rowp, r_rowp, s_dr, r_dr, s_dc, r_dc, s_y, r_y,
@@ -249,11 +250,17 @@
     side = jnp.where(lane == 2, live_own, side)
     mine_s[:, width:] = side.astype(BF16)
 
+    last = context(ql_ref[...], qml_ref[...], kt_ref, v_ref, pl.ds(0, rows))
+
     tile = min(256, rows)
 
     def mix_in(t):
         at = pl.ds(t * tile, tile)
-        return tok_ref[at, :].astype(F32) + jnp.dot(ctx_ref[at, :], wout_ref[...], preferred_element_type=F32)
+        if t == rows // tile - 1:
+            rest = jnp.concatenate([ctx_ref[pl.ds(t * tile, tile - TILE), :], last], axis=0)
+        else:
+            rest = ctx_ref[at, :]
+        return tok_ref[at, :].astype(F32) + jnp.dot(rest, wout_ref[...], preferred_element_type=F32)
 
     def norm(resid):
         centre = resid - jnp.sum(resid, axis=1, keepdims=True) * (1.0 / width)
@@ -361,7 +368,7 @@
             copy().wait_send()
 
 
-def contrast(counts, positives, seg, tokens, ctx, w_out, gain, w_proj, n_z, n_y, n_x):
+def contrast(counts, positives, seg, tokens, ctx, w_out, gain, w_proj, last, n_z, n_y, n_x):
     slots = positives.shape[1]
     n_a, n_b = n_z * 2, n_y * n_x
     width, embed = w_proj.shape
@@ -371,7 +378,7 @@
         functools.partial(loss_kernel, n_z, n_y, n_x, slots),
         name="contrast",
         out_shape=(jax.ShapeDtypeStruct((1, slots), F32), jax.ShapeDtypeStruct((slots, width), F32)),
-        in_specs=[vmem] * 8,
+        in_specs=[vmem] * 12,
         out_specs=(vmem, vmem),
         scratch_shapes=[
             pltpu.VMEM((slots, width + 128), BF16),
@@ -390,7 +397,7 @@
             *sems,
         ],
         compiler_params=pltpu.CompilerParams(collective_id=0, has_side_effects=True, vmem_limit_bytes=40 * 2**20),
-    )(counts, positives, seg, tokens, ctx, w_out, gain, w_proj)
+    )(counts, positives, seg, tokens, ctx, w_out, gain, w_proj, *last)
 
 
 def deliver_kernel(loss_ref, grad_ref, loss_hbm, grad_hbm, sem):
@@ -418,8 +425,8 @@
 def body(grid, tokens, seg_ids, counts, positives, w_qkv, w_out, ln_gain, w_proj):
     slots = positives.shape[0]
     in_hbm = functools.partial(pltpu.with_memory_space_constraint, memory_space=pltpu.HBM)
-    ctx, tokens, w_out, w_proj = attend(*map(in_hbm, (seg_ids, tokens, w_qkv, w_out, w_proj)), slots)
-    loss, grad = contrast(counts[None, :], positives[None, :], seg_ids, tokens, ctx, w_out, ln_gain[None, :], w_proj, *grid)
+    ctx, tokens, w_out, w_proj, *last = attend(*map(in_hbm, (seg_ids, tokens, w_qkv, w_out, w_proj)), slots)
+    loss, grad = contrast(counts[None, :], positives[None, :], seg_ids, tokens, ctx, w_out, ln_gain[None, :], w_proj, last, *grid)
     loss, grad = deliver(loss, grad)
     return loss.reshape(slots), grad
 

time: 45.2 us -> 44.8 us (level)
    pallas_call x1, Pallas kernels: 32.4 us -> 33.1 us  [contrast(): pl.pallas_call(functools.partial(loss_kernel, n_z, n_y, n_x, slots), name...]
    pallas_call x1, Pallas kernels: 11.4 us -> 10.7 us  [attend(): pl.pallas_call(functools.partial(attend_kernel, slots), name='attend', ou...]
where the time goes in v6:
time: 44.8 us; the launch traced here: 45.3 us
  Pallas kernels  44.5 us (99%)
  between operations  0.87 us (2%)
    pallas_call x1, Pallas kernels, contrast(): pl.pallas_call(functools.partial(loss_kernel, n_z, n_y, n_x, slots), name...  33.1 us
    pallas_call x1, Pallas kernels, attend(): pl.pallas_call(functools.partial(attend_kernel, slots), name='attend', ou...  10.7 us

profile of v6, /device:TPU:1, one launch (start us, length us, event | category | flops | bytes accessed | tf_op | source)
XLA Modules:
  0.0 45.3 jit_solution(14857969571638797501)
XLA Ops:
  0.6 0.0 copy-start
  0.6 0.0 copy-start.1
  0.7 0.0 copy-start.2
  0.7 0.0 copy-start.3
  0.7 10.7 %attend.1 = (bf16[1024,512]{1,0:T(8,128)(2,1)S(1)}, bf16[1024,1024]{1,0:T(8,128)(2,1)S(1)}, bf16[512,1024]{1,0:T(8,128)(2,1)S(1)}, bf16[1024,2048]{1,0:T(8,128)(...) custom-call(s32[1,1024]{1,0:T(1,128)} %seg_ref.1, ...), custom_call_target="tpu_custom_call" | custom-call | flops 8000000000 | bytes 6291456 | tf_op jit(solution)/shard_map/attend/pallas_call | solution.py:143
  11.4 0.0 copy-done
  11.4 0.0 copy-done.1
  11.4 0.0 copy-done.2
  11.4 0.0 copy-done.3
  11.4 33.1 %contrast.1 = (f32[1,4]{1,0:T(1,128)S(1)}, f32[4,1024]{1,0:T(4,128)S(1)}) custom-call(s32[1,256]{1,0:T(1,128)S(1)} %bitcast.5, s32[1,4]{1,0:T(1,128)S(1)} %bitcast.6, s32[1,1024]{1,0:T(1,128)S(1)} %copy-done, bf16[1024,1024]{1,0:T(8,128)(2,1)S(1)} %get-tuple-element.14.tok_ref, bf16[1024,512]{1,0:T(8,128)(2,1)S(1)} %get-tuple-element.15.ctx_ref, ...), custom_call_target="tpu_custom_call" | custom-call | tf_op jit(solution)/shard_map/contrast/pallas_call | solution.py:377
  44.6 0.6 %deliver.1 = (f32[1,4]{1,0:T(1,128)}, f32[4,1024]{1,0:T(4,128)}) custom-call(f32[1,4]{1,0:T(1,128)S(1)} %get-tuple-element.22.loss_ref, f32[4,1024]{1,0:T(4,128)S(1)} %get-tuple-element.23.grad_ref), custom_call_target="tpu_custom_call" | custom-call | tf_op jit(solution)/shard_map/deliver/pallas_call | solution.py:414
Async XLA Ops:
  0.6 10.7 %copy-start = (s32[1,1024]{1,0:T(1,128)S(1)}, s32[1,1024]{1,0:T(1,128)}, u32[]{:S(2)}) copy-start(s32[1,1024]{1,0:T(1,128)} %seg_ref.1) | copy-start | bytes 12292
  0.6 10.7 %copy-start.1 = (f32[1024]{0:T(1024)S(1)}, f32[1024]{0:T(1024)}, u32[]{:S(2)}) copy-start(f32[1024]{0:T(1024)} %param.14) | copy-start | bytes 12292
  0.7 10.7 %copy-start.2 = (s32[256]{0:T(256)S(1)}, s32[256]{0:T(256)}, u32[]{:S(2)}) copy-start(s32[256]{0:T(256)} %param.10) | copy-start | bytes 3076
  0.7 10.7 %copy-start.3 = (s32[4]{0:T(128)S(1)}, s32[4]{0:T(128)}, u32[]{:S(2)}) copy-start(s32[4]{0:T(128)} %param.11) | copy-start | bytes 52

commit v7 on v5

--- a/solution.py
+++ b/solution.py
@@ -258,7 +258,7 @@
     def norm(resid):
         centre = resid - jnp.sum(resid, axis=1, keepdims=True) * (1.0 / width)
         variance = jnp.sum(centre * centre, axis=1, keepdims=True) * (1.0 / width)
-        return (centre * lax.rsqrt(variance + 1e-05) * gain_ref[...]).astype(BF16)
+        return (centre * lax.rsqrt(variance + 1e-05)).astype(BF16)
 
     def pool(t, hidden):
         member = (iota((16, tile), 0) == seg_ref[:, pl.ds(t * tile, tile)]).astype(F32).astype(BF16)
@@ -267,7 +267,7 @@
     resids = [mix_in(t) for t in range(rows // tile)]
     sums = sum(pool(t, norm(resid)) for t, resid in enumerate(resids))
     sizes = jnp.sum((iota((16, rows), 0) == seg_ref[...]).astype(F32), axis=1, keepdims=True)
-    pooled = (sums[:slots] / sizes[:slots]).astype(BF16)
+    pooled = (sums[:slots] / sizes[:slots] * gain_ref[...]).astype(BF16)
     mine_s[:, :width] = pooled
 
     pl.semaphore_wait(barrier, n_a + n_b - 2)
@@ -286,16 +286,23 @@
     colp[a] = mine_s[...]
     rowp[b] = mine_s[...]
     p_s[...] = jnp.zeros_like(p_s)
+    emb_s[...] = jnp.zeros_like(emb_s)
+
+    def embed_rows(first, count):
+        at = pl.ds(first, count)
+        proj_at = jnp.dot(p_s[at, :width].astype(BF16), w_ref[...], preferred_element_type=F32)
+        rnorm_at = lax.rsqrt(jnp.sum(proj_at * proj_at, axis=1, keepdims=True) + 1e-06)
+        emb_s[at, :] = (proj_at * rnorm_at).astype(BF16)
+
     arrive(x_row)
     for o in range(n_b):
         p_s[128 + o * slots : 128 + (o + 1) * slots, :] = rowp[o].astype(F32)
+    embed_rows(128, r_rows)
     arrive(x_col)
     for o in range(n_a):
         p_s[o * slots : (o + 1) * slots, :] = colp[o].astype(F32)
 
-    proj_all = jnp.dot(p_s[:, :width].astype(BF16), w_ref[...], preferred_element_type=F32)
-    rnorm_all = lax.rsqrt(jnp.sum(proj_all * proj_all, axis=1, keepdims=True) + 1e-06)
-    emb_s[...] = (proj_all * rnorm_all).astype(BF16)
+    embed_rows(0, c_cols)
     emb_j = emb_s[:128, :]
     logits = SCALE * lax.dot_general(emb_s[128 : 128 + r_rows, :], emb_j, NT, preferred_element_type=F32)
 

time: 45.2 us -> 45.4 us (level)
    pallas_call x1, Pallas kernels: 11.4 us -> 13.6 us  [attend(): pl.pallas_call(functools.partial(attend_kernel, slots), name='attend', ou...]
    pallas_call x1, Pallas kernels: 32.4 us -> 30.5 us  [contrast(): pl.pallas_call(functools.partial(loss_kernel, n_z, n_y, n_x, slots), name...]
where the time goes in v7:
time: 45.4 us; the launch traced here: 45.7 us
  Pallas kernels  44.8 us (99%)
  between operations  0.87 us (2%)
    pallas_call x1, Pallas kernels, contrast(): pl.pallas_call(functools.partial(loss_kernel, n_z, n_y, n_x, slots), name...  30.5 us
    pallas_call x1, Pallas kernels, attend(): pl.pallas_call(functools.partial(attend_kernel, slots), name='attend', ou...  13.6 us

profile of v7, /device:TPU:1, one launch (start us, length us, event | category | flops | bytes accessed | tf_op | source)
XLA Modules:
  0.0 45.7 jit_solution(2975040186754570048)
XLA Ops:
  0.6 0.0 copy-start
  0.6 0.0 copy-start.1
  0.7 0.0 copy-start.2
  0.7 0.0 copy-start.3
  0.7 13.6 %attend.1 = (bf16[1024,512]{1,0:T(8,128)(2,1)S(1)}, bf16[1024,1024]{1,0:T(8,128)(2,1)S(1)}, bf16[512,1024]{1,0:T(8,128)(2,1)S(1)}, bf16[1024,2048]{1,0:T(8,128)(2,1)S(1)}) custom-call(s32[1,1024]{1,0:T(1,128)} %seg_ref.1, bf16[1024,1024]{1,0:T(8,128)(2,1)} %tok_hbm.1, bf16[1024,1536]{1,0:T(8,128)(2,1)} %wqkv_hbm.1, bf16[512,1024]{1,0:T(8,128)(2,1)} %wout_hbm.1, ...), custom_call_target="tpu_custom_call" | custom-call | flops 8000000000 | bytes 6291456 | tf_op jit(solution)/shard_map/attend/pallas_call | solution.py:147
  14.3 0.0 copy-done
  14.3 0.0 copy-done.1
  14.3 0.0 copy-done.2
  14.3 0.0 copy-done.3
  14.3 30.5 %contrast.1 = (f32[1,4]{1,0:T(1,128)S(1)}, f32[4,1024]{1,0:T(4,128)S(1)}) custom-call(s32[1,256]{1,0:T(1,128)S(1)} %bitcast.5, s32[1,4]{1,0:T(1,128)S(1)} %bitcast.6, s32[1,1024]{1,0:T(1,128)S(1)} %copy-done, bf16[1024,1024]{1,0:T(8,128)(2,1)S(1)} %get-tuple-element.10.tok_ref, bf16[1024,512]{1,0:T(8,128)(2,1)S(1)} %get-tuple-element.11.ctx_ref, ...), custom_call_target="tpu_custom_call" | custom-call | tf_op jit(solution)/shard_map/contrast/pallas_call | solution.py:377
  44.9 0.6 %deliver.1 = (f32[1,4]{1,0:T(1,128)}, f32[4,1024]{1,0:T(4,128)}) custom-call(f32[1,4]{1,0:T(1,128)S(1)} %get-tuple-element.14.loss_ref, f32[4,1024]{1,0:T(4,128)S(1)} %get-tuple-element.15.grad_ref), custom_call_target="tpu_custom_call" | custom-call | tf_op jit(solution)/shard_map/deliver/pallas_call | solution.py:414
Async XLA Ops:
  0.6 13.7 %copy-start = (s32[1,1024]{1,0:T(1,128)S(1)}, s32[1,1024]{1,0:T(1,128)}, u32[]{:S(2)}) copy-start(s32[1,1024]{1,0:T(1,128)} %seg_ref.1) | copy-start | bytes 12292
  0.6 13.7 %copy-start.1 = (f32[1024]{0:T(1024)S(1)}, f32[1024]{0:T(1024)}, u32[]{:S(2)}) copy-start(f32[1024]{0:T(1024)} %param.14) | copy-start | bytes 12292
  0.7 13.7 %copy-start.2 = (s32[256]{0:T(256)S(1)}, s32[256]{0:T(256)}, u32[]{:S(2)}) copy-start(s32[256]{0:T(256)} %param.10) | copy-start | bytes 3076
  0.7 13.7 %copy-start.3 = (s32[4]{0:T(128)S(1)}, s32[4]{0:T(128)}, u32[]{:S(2)}) copy-start(s32[4]{0:T(128)} %param.11) | copy-start | bytes 52

commit v8 on v5

--- a/solution.py
+++ b/solution.py
@@ -316,16 +316,17 @@
     pos_j, live_j = along(side_j[:, 0:1] * 32.0 + side_j[:, 1:2]), along(side_j[:, 2:3]) > 0.5
     inside = (c < c_cols) & (id_i != id_j)
     expd = jnp.exp(logits)
+    exp_j = jnp.where(inside & live_i, expd, 0.0)
+    mdc[...] = jnp.sum(exp_j, axis=0, keepdims=True)
+    start(x_dc)
     exp_i = jnp.where(inside & live_j, expd, 0.0)
-    exp_j = jnp.where(inside & live_i, expd, 0.0)
     hit_i = (pos_i == id_j.astype(F32)) & (c < c_cols)
     hit_j = (pos_j == id_i.astype(F32)) & (c < c_cols)
     part_i = jnp.sum(exp_i, axis=1, keepdims=True)
     picked = jnp.sum(jnp.where(hit_i, logits, 0.0), axis=1, keepdims=True)
-    mdc[...] = jnp.sum(exp_j, axis=0, keepdims=True)
     mdr[0:1, :] = jnp.sum(jnp.where(eye, part_i, 0.0), axis=0, keepdims=True)
     mdr[1:2, :] = jnp.sum(jnp.where(eye, picked, 0.0), axis=0, keepdims=True)
-    start(x_dr, x_dc)
+    start(x_dr)
     drow[b] = mdr[...]
     dcol[a] = mdc[...]
     arrive(x_dr)

time: 45.2 us -> 45.4 us (level); the launches traced: 45.3 us -> 45 us
    pallas_call x1, Pallas kernels: 32.4 us -> 31.1 us  [contrast(): pl.pallas_call(functools.partial(loss_kernel, n_z, n_y, n_x, slots), name...]
    pallas_call x1, Pallas kernels: 11.4 us -> 12.3 us  [attend(): pl.pallas_call(functools.partial(attend_kernel, slots), name='attend', ou...]
where the time goes in v8:
time: 45.4 us; the launch traced here: 45 us
  Pallas kernels  44.1 us (97%)
  between operations  0.87 us (2%)
    pallas_call x1, Pallas kernels, contrast(): pl.pallas_call(functools.partial(loss_kernel, n_z, n_y, n_x, slots), name...  31.1 us
    pallas_call x1, Pallas kernels, attend(): pl.pallas_call(functools.partial(attend_kernel, slots), name='attend', ou...  12.3 us

profile of v8, /device:TPU:1, one launch (start us, length us, event | category | flops | bytes accessed | tf_op | source)
XLA Modules:
  0.0 45.0 jit_solution(4427850580381736798)
XLA Ops:
  0.6 0.0 copy-start
  0.6 0.0 copy-start.1
  0.7 0.0 copy-start.2
  0.7 0.0 copy-start.3
  0.7 12.3 %attend.1 = (bf16[1024,512]{1,0:T(8,128)(2,1)S(1)}, bf16[1024,1024]{1,0:T(8,128)(2,1)S(1)}, bf16[512,1024]{1,0:T(8,128)(2,1)S(1)}, bf16[1024,2048]{1,0:T(8,128)(2,1)S(1)}) custom-call(s32[1,1024]{1,0:T(1,128)} %seg_ref.1, bf16[1024,1024]{1,0:T(8,128)(2,1)} %tok_hbm.1, bf16[1024,1536]{1,0:T(8,128)(2,1)} %wqkv_hbm.1, bf16[512,1024]{1,0:T(8,128)(2,1)} %wout_hbm.1, ...), custom_call_target="tpu_custom_call" | custom-call | flops 8000000000 | bytes 6291456 | tf_op jit(solution)/shard_map/attend/pallas_call | solution.py:147
  13.0 0.0 copy-done
  13.0 0.0 copy-done.1
  13.0 0.0 copy-done.2
  13.0 0.0 copy-done.3
  13.0 31.1 %contrast.1 = (f32[1,4]{1,0:T(1,128)S(1)}, f32[4,1024]{1,0:T(4,128)S(1)}) custom-call(s32[1,256]{1,0:T(1,128)S(1)} %bitcast.5, s32[1,4]{1,0:T(1,128)S(1)} %bitcast.6, s32[1,1024]{1,0:T(1,128)S(1)} %copy-done, bf16[1024,1024]{1,0:T(8,128)(2,1)S(1)} %get-tuple-element.10.tok_ref, bf16[1024,512]{1,0:T(8,128)(2,1)S(1)} %get-tuple-element.11.ctx_ref, ...), custom_call_target="tpu_custom_call" | custom-call | tf_op jit(solution)/shard_map/contrast/pallas_call | solution.py:371
  44.2 0.6 %deliver.1 = (f32[1,4]{1,0:T(1,128)}, f32[4,1024]{1,0:T(4,128)}) custom-call(f32[1,4]{1,0:T(1,128)S(1)} %get-tuple-element.14.loss_ref, f32[4,1024]{1,0:T(4,128)S(1)} %get-tuple-element.15.grad_ref), custom_call_target="tpu_custom_call" | custom-call | tf_op jit(solution)/shard_map/deliver/pallas_call | solution.py:408
Async XLA Ops:
  0.6 12.3 %copy-start = (s32[1,1024]{1,0:T(1,128)S(1)}, s32[1,1024]{1,0:T(1,128)}, u32[]{:S(2)}) copy-start(s32[1,1024]{1,0:T(1,128)} %seg_ref.1) | copy-start | bytes 12292
  0.6 12.3 %copy-start.1 = (f32[1024]{0:T(1024)S(1)}, f32[1024]{0:T(1024)}, u32[]{:S(2)}) copy-start(f32[1024]{0:T(1024)} %param.14) | copy-start | bytes 12292
  0.7 12.3 %copy-start.2 = (s32[256]{0:T(256)S(1)}, s32[256]{0:T(256)}, u32[]{:S(2)}) copy-start(s32[256]{0:T(256)} %param.10) | copy-start | bytes 3076
  0.7 12.3 %copy-start.3 = (s32[4]{0:T(128)S(1)}, s32[4]{0:T(128)}, u32[]{:S(2)}) copy-start(s32[4]{0:T(128)} %param.11) | copy-start | bytes 52
